TPU v7x, 256 devices: a whole 4x4x8 slice. The times are simulated.
256 devices in a mesh: beam: 32 (over x, y, core), grp: 8 (over z).
Axes of the slice: x: 4, y: 4, z: 8, core: 2. Of those that a mesh axis runs over, the one named last changes fastest.
Arguments:
- beam_data: bfloat16 [2, 16384, 256], P(None, 'beam', 'grp'), may hold values from -6 to 6
- window_count: int32 [256], P(('beam', 'grp')), may hold values from 1 to 8
- slot_owner: int32 [256, 8, 1], P(('beam', 'grp')), may hold values from 0 to 31; in each aligned block of 8 rows (0 to 7, 8 to 15, ..., all dimensions but the last counted through in order) at most 2 rows name the same one
- slot_window: int32 [256, 8], P(('beam', 'grp')), may hold values from 0 to 3
- grid_index: int32 [256, 4096], P(('beam', 'grp')), may hold values from 0 to 4095
Outputs:
- spectrum: float32 [256, 4096], P(('beam', 'grp'))
Inputs may be any that keep to these rules, and one draw needn't show every extreme that they name: a user's slots 0 to window_count - 1 are live. `slot_owner`: among the 8 slots of the users of one device no owner is named more than 2 times, a bound that some block reaches.
All inputs are finite; a program needn't handle non-finite values.
Results may differ from a plain program's by a relative error of at most 0.0003.
Values may be sent and summed in bfloat16 or wider, within the bound.
A program may use at most 64 MiB of HBM per device.

v0:
```python
import jax
import jax.numpy as jnp
from jax import lax
from jax.sharding import PartitionSpec as P

WIN_BEAMS = 128
NOISE_DIM = 64
SNAPS = 256
OVERSAMPLE = 32
ITERS = 8


highest = lax.Precision.HIGHEST
shift_factor = 1.05
spectral_floor = 0.05


def total_of_pieces(value, axis):
    blocks = lax.all_gather(value, axis)
    return blocks.sum(axis=0)


def orthonormal(image_block):
    gram_matrix = jnp.einsum(
        "uic,uid->ucd",
        image_block,
        image_block,
        precision=highest,
        preferred_element_type=jnp.float32,
    )
    lower_factor = jnp.linalg.cholesky(gram_matrix)

    def solve_one(factor, matrix):
        return jax.scipy.linalg.solve_triangular(factor, matrix.T, lower=True)

    solved = jax.vmap(solve_one)(lower_factor, image_block)
    return jnp.swapaxes(solved, 1, 2)


def steering(grid_rows, beams_total):
    position = (grid_rows.astype(jnp.float32) + 0.5) / OVERSAMPLE
    offset = position[..., None] - jnp.arange(WIN_BEAMS, dtype=jnp.float32)
    turned = jnp.pi * offset
    magnitude = jnp.sin(turned) / (beams_total * jnp.sin(turned / beams_total))
    phase_angle = turned * ((beams_total - 1) / beams_total)
    return jnp.concatenate(
        [magnitude * jnp.cos(phase_angle), magnitude * jnp.sin(phase_angle)], axis=-1
    )


def owner_slots(owners, locals_flat, beam_count, slot_cap):
    owner_hits = (owners[:, None] == jnp.arange(beam_count, dtype=jnp.int32)[None, :]).astype(
        jnp.int32
    )
    earlier = jnp.cumsum(owner_hits, axis=0) - owner_hits
    order_in = jnp.sum(earlier * owner_hits, axis=1)
    slot_match = owner_hits[:, :, None] * (
        order_in[:, None, None] == jnp.arange(slot_cap, dtype=jnp.int32)[None, None, :]
    ).astype(jnp.int32)
    requests = jnp.sum(slot_match * locals_flat[:, None, None], axis=0)
    return (requests, owners * slot_cap + order_in)


def pack_upper(same_part, imag_part):
    width = same_part.shape[-1]
    row_ids = jnp.arange(width, dtype=jnp.int32)[:, None]
    col_ids = jnp.arange(width, dtype=jnp.int32)[None, :]
    return jnp.where((row_ids <= col_ids)[None], same_part, imag_part)


def packed_sums(picked_packed, counts, slot_count):
    live_mask = (jnp.arange(slot_count, dtype=jnp.int32)[None, :] < counts[:, None]).astype(
        jnp.float32
    )
    packed_sum = jnp.einsum("uk,ukij->uij", live_mask, picked_packed, precision=highest)
    flipped = jnp.swapaxes(packed_sum, 1, 2)
    width = packed_sum.shape[-1]
    row_ids = jnp.arange(width, dtype=jnp.int32)[:, None]
    col_ids = jnp.arange(width, dtype=jnp.int32)[None, :]
    same_sum = jnp.where((row_ids <= col_ids)[None], packed_sum, flipped)
    imag_sum = jnp.where(
        (row_ids > col_ids)[None], packed_sum, jnp.where((row_ids < col_ids)[None], -flipped, 0.0)
    )
    return (same_sum, imag_sum)


def local_grams(window_view):
    same_part = jnp.einsum(
        "wis,wjs->wij", window_view[0], window_view[0], preferred_element_type=jnp.float32
    )
    same_part = same_part + jnp.einsum(
        "wis,wjs->wij", window_view[1], window_view[1], preferred_element_type=jnp.float32
    )
    cross_part = jnp.einsum(
        "wis,wjs->wij", window_view[1], window_view[0], preferred_element_type=jnp.float32
    )
    return (same_part, cross_part)


def finish_users(same_sum, imag_sum, counts, grid_index, beams_total):
    inverse_count = 1.0 / (counts.astype(jnp.float32) * SNAPS)
    top_rows = jnp.concatenate([same_sum, -imag_sum], axis=2)
    bottom_rows = jnp.concatenate([imag_sum, same_sum], axis=2)
    covariance = jnp.concatenate([top_rows, bottom_rows], axis=1) * inverse_count[:, None, None]
    square = jnp.einsum(
        "uij,ujk->uik",
        covariance,
        covariance,
        precision=highest,
        preferred_element_type=jnp.float32,
    )
    fourth = jnp.einsum(
        "uij,ujk->uik", square, square, precision=highest, preferred_element_type=jnp.float32
    )
    shift_value = shift_factor * jnp.sqrt(jnp.sqrt(jnp.sqrt(jnp.sum(fourth * fourth, axis=(1, 2)))))
    shifted = shift_value[:, None, None] * jnp.eye(2 * WIN_BEAMS, dtype=jnp.float32) - covariance
    start_block = jnp.concatenate(
        [shifted[:, :, :NOISE_DIM], shifted[:, :, WIN_BEAMS : WIN_BEAMS + NOISE_DIM]], axis=2
    )
    noise_basis = orthonormal(start_block)
    for sweep in range(ITERS - 1):
        noise_basis = orthonormal(
            jnp.einsum(
                "uij,ujc->uic",
                shifted,
                noise_basis,
                precision=highest,
                preferred_element_type=jnp.float32,
            )
        )
    steering_rows = steering(grid_index, beams_total)
    projected = jnp.einsum(
        "ugc,ucq->ugq",
        steering_rows,
        noise_basis,
        precision=highest,
        preferred_element_type=jnp.float32,
    )
    leakage = jnp.sum(projected * projected, axis=-1) / jnp.sum(
        steering_rows * steering_rows, axis=-1
    )
    return 1.0 / (leakage + spectral_floor)


def local(beam_data, window_count, slot_owner, slot_window, grid_index):
    beam_count = lax.axis_size("beam")
    user_count = window_count.shape[0]
    slot_count = slot_window.shape[1]
    window_width = WIN_BEAMS
    local_windows = beam_data.shape[1] // window_width
    slot_cap = (user_count * slot_count + beam_count - 1) // beam_count + 1
    beams_total = beam_data.shape[1] * beam_count
    snap_local = beam_data.shape[2]
    owners = slot_owner[:, :, 0]
    window_view = beam_data.reshape(2, local_windows, window_width, snap_local)
    same_part, cross_part = local_grams(window_view)
    packed_part = pack_upper(same_part, cross_part - jnp.swapaxes(cross_part, 1, 2))
    window_packed = total_of_pieces(packed_part, "grp")
    requests, flat_slot = owner_slots(
        owners.reshape(-1), slot_window.reshape(-1), beam_count, slot_cap
    )
    picked = jnp.take(
        window_packed,
        lax.all_to_all(requests, "beam", split_axis=0, concat_axis=0, tiled=True),
        axis=0,
    )
    got_packed = lax.all_to_all(picked, "beam", split_axis=0, concat_axis=0, tiled=True)
    picked_packed = jnp.take(
        got_packed.reshape(beam_count * slot_cap, window_width, window_width), flat_slot, axis=0
    )
    picked_packed = picked_packed.reshape(user_count, slot_count, window_width, window_width)
    same_sum, imag_sum = packed_sums(picked_packed, window_count, slot_count)
    return finish_users(same_sum, imag_sum, window_count, grid_index, beams_total)


def solution(mesh):
    placed = (
        P(None, "beam", "grp"),
        P(("beam", "grp")),
        P(("beam", "grp"), None, None),
        P(("beam", "grp"), None),
        P(("beam", "grp"), None),
    )
    return jax.shard_map(
        local, mesh=mesh, in_specs=placed, out_specs=P(("beam", "grp"), None), check_vma=False
    )
```

profile of v0, /device:TPU:1, one launch (start us, length us, event | category | flops | bytes accessed | tf_op | source)
XLA Modules:
  0.0 336.1 jit_solution(574163317017402806)
XLA Ops:
  6.6 0.8 fusion.97
  8.0 1.0 fusion.6
  9.5 15.3 %all_to_all.20 = s32[32,1,2]{2,1,0:T(1,128)S(1)} all-to-all(s32[32,1,2]{2,1,0:T(1,128)S(1)} %copy.81), channel_id=1, replica_groups=mesh['beam'=32,'grp'=8] {'beam'}, dimensions={0} | all-to-all | bytes 512 | tf_op jit(solution)/shard_map/all_to_all | solution.py:164
  25.2 24.4 %all-gather.3.cloned.1.call-done = f32[32,128,128]{2,1,0:T(8,128)} async-done(((f32[4,128,128]{2,1,0:T(8,128)}), f32[32,128,128]{2,1,0:T(8,128)}) %all-gather.3.cloned.1.call-update) | async-done | bytes 2097168 | tf_op jit(solution)/shard_map/all_gather | solution.py:19
  49.6 1.7 reduce_sum.58
  51.3 2.8 gather_fusion
  54.1 4.5 %broadcast_select_fusion = f32[32,2,128,128]{3,2,1,0:T(8,128)} fusion(f32[32,2,128,128]{3,2,1,0:T(8,128)} %bitcast.238, pred[32,2]{1,0:T(8,128)(4,1)S(1)} %copy.83), kind=kLoop, calls=%fused_computation.13 | loop fusion | flops 1048576 | bytes 8388672 | tf_op jit(solution)/shard_map/jit(_take)/select_n | solution.py:162
  58.5 12.6 %all-to-all-start.1 = ((f32[32,2,128,128]{3,2,1,0:T(8,128)}), f32[32,2,128,128]{3,2,1,0:T(8,128)}, u32[]{:S(2)}, u32[]{:S(2)}) async-start(f32[32,2,128,128]{3,2,1,0:T(8,128)} %broadcast_select_fusion), calls=%async_computation.1 | async-start | bytes 8388608 | tf_op jit(solution)/shard_map/all_to_all | solution.py:167
  71.9 21.2 %multiply_bitcast_fusion.1 = (f32[1,4096,128]{2,1,0:T(8,128)S(1)}, f32[1,4096,128]{2,1,0:T(8,128)S(1)}) fusion(f32[4096]{0:T(1024)S(1)} %bitcast.250), kind=kLoop, calls=%fused_computation.9 | loop fusion | flops 4194304 | bytes 4210688 | tf_op jit(solution)/shard_map/concatenate | solution.py:46
  93.1 0.6 fusion.2
  93.8 23.3 %cosine_multiply_fusion = (f32[1,4096,128]{2,1,0:T(8,128)S(1)}, f32[1,4096,128]{2,1,0:T(8,128)}) fusion(f32[4096]{0:T(1024)S(1)} %bitcast.251), kind=kLoop, calls=%fused_computation.15 | loop fusion | flops 4194304 | bytes 4210688 | tf_op jit(solution)/shard_map/mul | solution.py:47
  117.0 6.0 %all-to-all-done.1 = f32[32,2,128,128]{3,2,1,0:T(8,128)} async-done(((f32[32,2,128,128]{3,2,1,0:T(8,128)}), f32[32,2,128,128]{3,2,1,0:T(8,128)}, u32[]{:S(2)}, u32[]{:S(2)}) %all-to-all-start.1) | async-done | bytes 4194336 | tf_op jit(solution)/shard_map/all_to_all | solution.py:167
  123.1 2.8 gather_fusion.1
  126.0 0.6 fusion.8
  127.2 1.0 fusion.7
  129.6 11.7 %custom-call.20 = f32[1,128,128]{2,1,0:T(8,128)S(1)} custom-call(f32[1,128,128]{2,1,0:T(8,128)S(1)} %fusion.46), custom_call_target="Cholesky" | custom-call | tf_op jit(solution)/shard_map/jit(cholesky)/cholesky | solution.py:31
  141.3 0.6 compare_reduce_fusion.7
  142.0 0.7 fusion.31
  142.7 9.8 %custom-call.21 = f32[1,1,128,128]{2,3,1,0:T(8,128)S(1)} custom-call(f32[1,1,128,128]{3,2,1,0:T(8,128)S(1)} %fusion.31), custom_call_target="InvertDiagBlocksLowerTriangular" | custom-call | tf_op jit(solution)/shard_map/vmap(jit(_solve_triangular))/triangular_solve | solution.py:34
  153.7 12.1 %custom-call.22 = f32[1,128,128]{2,1,0:T(8,128)S(1)} custom-call(f32[1,128,128]{2,1,0:T(8,128)S(1)} %fusion.45), custom_call_target="Cholesky" | custom-call | tf_op jit(solution)/shard_map/jit(cholesky)/cholesky | solution.py:31
  165.8 0.6 compare_reduce_fusion.6
  166.5 0.7 fusion.32
  167.2 9.8 %custom-call.23 = f32[1,1,128,128]{2,3,1,0:T(8,128)S(1)} custom-call(f32[1,1,128,128]{3,2,1,0:T(8,128)S(1)} %fusion.32), custom_call_target="InvertDiagBlocksLowerTriangular" | custom-call | tf_op jit(solution)/shard_map/vmap(jit(_solve_triangular))/triangular_solve | solution.py:34
  178.2 11.7 %custom-call.24 = f32[1,128,128]{2,1,0:T(8,128)S(1)} custom-call(f32[1,128,128]{2,1,0:T(8,128)S(1)} %fusion.44), custom_call_target="Cholesky" | custom-call | tf_op jit(solution)/shard_map/jit(cholesky)/cholesky | solution.py:31
  189.9 0.6 compare_reduce_fusion.5
  190.6 0.7 fusion.33
  191.2 9.8 %custom-call.25 = f32[1,1,128,128]{2,3,1,0:T(8,128)S(1)} custom-call(f32[1,1,128,128]{3,2,1,0:T(8,128)S(1)} %fusion.33), custom_call_target="InvertDiagBlocksLowerTriangular" | custom-call | tf_op jit(solution)/shard_map/vmap(jit(_solve_triangular))/triangular_solve | solution.py:34
  202.3 11.9 %custom-call.26 = f32[1,128,128]{2,1,0:T(8,128)S(1)} custom-call(f32[1,128,128]{2,1,0:T(8,128)S(1)} %fusion.43), custom_call_target="Cholesky" | custom-call | tf_op jit(solution)/shard_map/jit(cholesky)/cholesky | solution.py:31
  214.2 0.6 compare_reduce_fusion.4
  214.8 0.7 fusion.34
  215.5 9.8 %custom-call.27 = f32[1,1,128,128]{2,3,1,0:T(8,128)S(1)} custom-call(f32[1,1,128,128]{3,2,1,0:T(8,128)S(1)} %fusion.34), custom_call_target="InvertDiagBlocksLowerTriangular" | custom-call | tf_op jit(solution)/shard_map/vmap(jit(_solve_triangular))/triangular_solve | solution.py:34
  226.5 11.7 %custom-call.28 = f32[1,128,128]{2,1,0:T(8,128)S(1)} custom-call(f32[1,128,128]{2,1,0:T(8,128)S(1)} %fusion.42), custom_call_target="Cholesky" | custom-call | tf_op jit(solution)/shard_map/jit(cholesky)/cholesky | solution.py:31
  238.2 0.6 compare_reduce_fusion.3
  238.9 0.7 fusion.35
  239.5 10.2 %custom-call.29 = f32[1,1,128,128]{2,3,1,0:T(8,128)S(1)} custom-call(f32[1,1,128,128]{3,2,1,0:T(8,128)S(1)} %fusion.35), custom_call_target="InvertDiagBlocksLowerTriangular" | custom-call | tf_op jit(solution)/shard_map/vmap(jit(_solve_triangular))/triangular_solve | solution.py:34
  250.9 11.7 %custom-call.30 = f32[1,128,128]{2,1,0:T(8,128)S(1)} custom-call(f32[1,128,128]{2,1,0:T(8,128)S(1)} %fusion.41), custom_call_target="Cholesky" | custom-call | tf_op jit(solution)/shard_map/jit(cholesky)/cholesky | solution.py:31
  262.7 0.6 compare_reduce_fusion.2
  263.3 0.7 fusion.36
  264.0 9.8 %custom-call.31 = f32[1,1,128,128]{2,3,1,0:T(8,128)S(1)} custom-call(f32[1,1,128,128]{3,2,1,0:T(8,128)S(1)} %fusion.36), custom_call_target="InvertDiagBlocksLowerTriangular" | custom-call | tf_op jit(solution)/shard_map/vmap(jit(_solve_triangular))/triangular_solve | solution.py:34
  275.0 11.7 %custom-call.32 = f32[1,128,128]{2,1,0:T(8,128)S(1)} custom-call(f32[1,128,128]{2,1,0:T(8,128)S(1)} %fusion.40), custom_call_target="Cholesky" | custom-call | tf_op jit(solution)/shard_map/jit(cholesky)/cholesky | solution.py:31
  286.8 0.6 compare_reduce_fusion.1
  287.4 0.7 fusion.37
  288.1 9.9 %custom-call.33 = f32[1,1,128,128]{2,3,1,0:T(8,128)S(1)} custom-call(f32[1,1,128,128]{3,2,1,0:T(8,128)S(1)} %fusion.37), custom_call_target="InvertDiagBlocksLowerTriangular" | custom-call | tf_op jit(solution)/shard_map/vmap(jit(_solve_triangular))/triangular_solve | solution.py:34
  299.2 11.7 %custom-call.34 = f32[1,128,128]{2,1,0:T(8,128)S(1)} custom-call(f32[1,128,128]{2,1,0:T(8,128)S(1)} %fusion.39), custom_call_target="Cholesky" | custom-call | tf_op jit(solution)/shard_map/jit(cholesky)/cholesky | solution.py:31
  311.0 0.6 compare_reduce_fusion
  311.6 0.7 fusion.38
  312.3 9.8 %custom-call.35 = f32[1,1,128,128]{2,3,1,0:T(8,128)S(1)} custom-call(f32[1,1,128,128]{3,2,1,0:T(8,128)S(1)} %fusion.38), custom_call_target="InvertDiagBlocksLowerTriangular" | custom-call | tf_op jit(solution)/shard_map/vmap(jit(_solve_triangular))/triangular_solve | solution.py:34
  322.4 6.0 %fusion.5 = f32[4096]{0:T(1024)S(1)} fusion(f32[128,256]{1,0:T(8,128)S(1)} %fusion.12, f32[1,4096,128]{2,1,0:T(8,128)} %get-tuple-element.19, f32[1,4096,128]{2,1,0:T(8,128)S(1)} %get-tuple-element.18), kind=kOutput, calls=%fused_computation.19 | convolution fusion | flops 1612705792 | bytes 4341760 | tf_op jit(solution)/shard_map/ugc,ucq->ugq/dot_general | solution.py:132
  (86 shorter events, 12.3 us)
Async XLA Ops:
  6.5 2.5 copy-start.1
  6.5 2.8 copy-start.2
  6.5 43.0 %all-gather.3.cloned.1.call-start = ((), (), s32[]{:S(2)}) async-start(), calls=%async_computation.2 | async-start | bytes 2359296 | tf_op jit(solution)/shard_map/all_gather | solution.py:19
  58.5 13.3 %copy-start = (s32[1,4096]{1,0:T(1,128)S(1)}, s32[1,4096]{1,0:T(1,128)}, u32[]{:S(2)}) copy-start(s32[1,4096]{1,0:T(1,128)} %param.12) | copy-start | bytes 49156
  58.5 64.5 %all-to-all-start.1 = ((f32[32,2,128,128]{3,2,1,0:T(8,128)}), f32[32,2,128,128]{3,2,1,0:T(8,128)}, u32[]{:S(2)}, u32[]{:S(2)}) async-start(f32[32,2,128,128]{3,2,1,0:T(8,128)} %broadcast_select_fusion), calls=%async_computation.1 | async-start | bytes 8388608 | tf_op jit(solution)/shard_map/all_to_all | solution.py:167
Sparse Core Ops, SparseCore 0:
  9.1 40.4 all-gather.2
where the time goes:
time: 339 us; the launch traced here: 336 us
  other arithmetic  236 us (70%)
  waiting for transfers between devices  30.4 us (9%)
  matrix products  17.9 us (5%)
  between operations  15.7 us (5%)
  blocking collectives  15.3 us (5%)
  starting transfers between devices  12.6 us (4%)
  local copies, waits for them, and re-layouts  7.79 us (2%)
    another operation x24, other arithmetic, orthonormal(): lower_factor = jnp.linalg.cholesky(gram_matrix)  99.6 us
    another operation x16, other arithmetic, solve_one(): return jax.scipy.linalg.solve_triangular(factor, matrix.T, lower=True)  84.2 us
    all_gather x1, waiting for transfers between devices, total_of_pieces(): blocks = lax.all_gather(value, axis)  24.4 us
    mul x1, other arithmetic, steering(): magnitude * jnp.cos(phase_angle)  23.3 us
    concatenate x1, other arithmetic, steering(): jnp.concatenate([magnitude * jnp.cos(phase_angle), magnitude * jnp.sin(ph...  21.2 us
    all_to_all x1, blocking collectives, local(): lax.all_to_all(requests, 'beam', split_axis=0, concat_axis=0, tiled=True)  15.3 us
    all_to_all x1, starting transfers between devices, local(): lax.all_to_all(picked, 'beam', split_axis=0, concat_axis=0, tiled=True)  12.6 us
  transfers between devices with their start and end apart: 2, of which 2 were waited for; matrix products, arithmetic and copies ran while one was open for 14% of the time, Pallas kernels for 0%

commit v1 on v0

v1 whole, which is shorter than its diff:
```python
import functools

import jax
import jax.numpy as jnp
from jax import lax
from jax.experimental import pallas as pl
from jax.experimental.pallas import tpu as pltpu
from jax.sharding import PartitionSpec as P

WIN_BEAMS = 128
NOISE_DIM = 64
SNAPS = 256
OVERSAMPLE = 32
ITERS = 8


highest = lax.Precision.HIGHEST
shift_factor = 1.05
spectral_floor = 0.05


def total_of_pieces(value, axis):
    blocks = lax.all_gather(value, axis)
    return blocks.sum(axis=0)


def owner_slots(owners, locals_flat, beam_count, slot_cap):
    owner_hits = (owners[:, None] == jnp.arange(beam_count, dtype=jnp.int32)[None, :]).astype(
        jnp.int32
    )
    earlier = jnp.cumsum(owner_hits, axis=0) - owner_hits
    order_in = jnp.sum(earlier * owner_hits, axis=1)
    slot_match = owner_hits[:, :, None] * (
        order_in[:, None, None] == jnp.arange(slot_cap, dtype=jnp.int32)[None, None, :]
    ).astype(jnp.int32)
    requests = jnp.sum(slot_match * locals_flat[:, None, None], axis=0)
    return (requests, owners * slot_cap + order_in)


def pack_upper(same_part, imag_part):
    width = same_part.shape[-1]
    row_ids = jnp.arange(width, dtype=jnp.int32)[:, None]
    col_ids = jnp.arange(width, dtype=jnp.int32)[None, :]
    return jnp.where((row_ids <= col_ids)[None], same_part, imag_part)


def local_grams(window_view):
    same_part = jnp.einsum(
        "wis,wjs->wij", window_view[0], window_view[0], preferred_element_type=jnp.float32
    )
    same_part = same_part + jnp.einsum(
        "wis,wjs->wij", window_view[1], window_view[1], preferred_element_type=jnp.float32
    )
    cross_part = jnp.einsum(
        "wis,wjs->wij", window_view[1], window_view[0], preferred_element_type=jnp.float32
    )
    return (same_part, cross_part)


GROW = (3.4445, -4.7750, 2.0315)
CLOSE = ((3.109266, -3.792034, 1.535381), (1.90467, -1.282586, 0.3782733), (1.875, -1.25, 0.375))
EXTRA = 6
CHUNK = 512


def halves(value):
    high = value.astype(jnp.bfloat16)
    return high, (value - high.astype(jnp.float32)).astype(jnp.bfloat16)


def dot(left, right):
    return jnp.dot(left, right, preferred_element_type=jnp.float32)


def dot_nt(left, right):
    return lax.dot_general(
        left, right, (((1,), (1,)), ((), ())), preferred_element_type=jnp.float32
    )


def product(left, right):
    return dot(left[0], right[0]) + (dot(left[0], right[1]) + dot(left[1], right[0]))


def product_half(left, right):
    both = dot(
        jnp.concatenate([left[0], left[1]], axis=1),
        jnp.concatenate([right[0], right[0]], axis=0),
    )
    return both + dot(left[0], right[1])


def whole(top):
    n = WIN_BEAMS
    return jnp.concatenate([top, jnp.concatenate([-top[:, n:], top[:, :n]], axis=1)], axis=0)


def finish_kernel(beams_total, packed_ref, count_ref, grid_ref, out_ref, a_hi, a_lo, w_ref):
    n = WIN_BEAMS
    row = lax.broadcasted_iota(jnp.int32, (n, n), 0)
    col = lax.broadcasted_iota(jnp.int32, (n, n), 1)
    packed = packed_ref[...]
    flipped = packed.T
    same = jnp.where(row <= col, packed, flipped)
    imag = jnp.where(row > col, packed, jnp.where(row < col, -flipped, 0.0))
    scale = jnp.full((1, 1), 1.0, jnp.float32) / (count_ref[0].astype(jnp.float32) * SNAPS)
    top = jnp.concatenate([same, -imag], axis=1) * scale
    square = product(halves(top), halves(whole(top)))
    fourth = product(halves(square), halves(whole(square)))
    power = 2.0 * jnp.sum(fourth * fourth, axis=(0, 1), keepdims=True)
    shift = shift_factor * jnp.sqrt(jnp.sqrt(jnp.sqrt(power)))
    row2 = lax.broadcasted_iota(jnp.int32, (n, 2 * n), 0)
    col2 = lax.broadcasted_iota(jnp.int32, (n, 2 * n), 1)
    shifted = whole(jnp.where(row2 == col2, 1.0, 0.0) - top / shift)
    hi, lo = halves(shifted)
    a_hi[...] = hi
    a_lo[...] = lo
    w_ref[...] = jnp.concatenate([shifted[:NOISE_DIM], shifted[n : n + NOISE_DIM]], axis=0)
    eye = jnp.where(row == col, 1.0, 0.0)

    def step(coefs, apply_a, precise):
        a, b, c = coefs
        basis = w_ref[...]
        parts = halves(basis)
        gram = dot_nt(parts[0], parts[0])
        if precise:
            gram = gram + (dot_nt(parts[0], parts[1]) + dot_nt(parts[1], parts[0]))
            gram_parts = halves(gram)
            gram2 = product_half(gram_parts, gram_parts)
        else:
            low = gram.astype(jnp.bfloat16)
            gram2 = dot(low, low)
        if apply_a:
            moved = halves(product(parts, (a_hi[...], a_lo[...])))
        else:
            moved = parts
        mix = halves(a * eye + b * gram + c * gram2)
        w_ref[...] = product_half(mix, moved)

    @pl.loop(0, ITERS - 1)
    def _(_):
        step(GROW, True, False)

    @pl.loop(0, EXTRA)
    def _(_):
        step(GROW, False, False)

    step(CLOSE[0], False, False)
    step(CLOSE[1], False, False)
    step(CLOSE[2], False, True)
    basis = w_ref[...]
    slope = jnp.pi / beams_total
    bias = -slope * jnp.sum(basis[:, n:], axis=1, keepdims=True)
    lead = halves(basis[:, :n])

    @pl.loop(0, grid_ref.shape[1] // CHUNK)
    def _(i):
        where = pl.ds(pl.multiple_of(i * CHUNK, CHUNK), CHUNK)
        position = (grid_ref[:, where].astype(jnp.float32) + 0.5) / OVERSAMPLE
        offset = position - lax.broadcasted_iota(jnp.int32, (n, CHUNK), 0).astype(jnp.float32)
        angle = (slope * offset) * (slope * offset)
        cot = 1.0 / offset - (slope * slope * offset) * (1.0 / 3.0 + angle * (1.0 / 45.0 + angle * (2.0 / 945.0)))
        projected = product_half(lead, halves(cot)) + bias
        energy = jnp.sum(projected * projected, axis=0, keepdims=True)
        length = jnp.sum(cot * cot, axis=0, keepdims=True) + n * slope * slope
        out_ref[:, where] = 1.0 / (energy / length + spectral_floor)


def finish_user(packed, count, grid_index, beams_total):
    n = WIN_BEAMS
    vmem = pl.BlockSpec(memory_space=pltpu.VMEM)
    return pl.pallas_call(
        functools.partial(finish_kernel, beams_total),
        out_shape=jax.ShapeDtypeStruct(grid_index.shape, jnp.float32),
        in_specs=[vmem, pl.BlockSpec(memory_space=pltpu.SMEM), vmem],
        out_specs=vmem,
        scratch_shapes=[
            pltpu.VMEM((2 * n, 2 * n), jnp.bfloat16),
            pltpu.VMEM((2 * n, 2 * n), jnp.bfloat16),
            pltpu.VMEM((n, 2 * n), jnp.float32),
        ],
        name="finish_user",
    )(packed, count, grid_index)


def local(beam_data, window_count, slot_owner, slot_window, grid_index):
    beam_count = lax.axis_size("beam")
    user_count = window_count.shape[0]
    slot_count = slot_window.shape[1]
    window_width = WIN_BEAMS
    local_windows = beam_data.shape[1] // window_width
    slot_cap = (user_count * slot_count + beam_count - 1) // beam_count + 1
    beams_total = beam_data.shape[1] * beam_count
    snap_local = beam_data.shape[2]
    owners = slot_owner[:, :, 0]
    window_view = beam_data.reshape(2, local_windows, window_width, snap_local)
    same_part, cross_part = local_grams(window_view)
    packed_part = pack_upper(same_part, cross_part - jnp.swapaxes(cross_part, 1, 2))
    window_packed = total_of_pieces(packed_part, "grp")
    requests, flat_slot = owner_slots(
        owners.reshape(-1), slot_window.reshape(-1), beam_count, slot_cap
    )
    picked = jnp.take(
        window_packed,
        lax.all_to_all(requests, "beam", split_axis=0, concat_axis=0, tiled=True),
        axis=0,
    )
    got_packed = lax.all_to_all(picked, "beam", split_axis=0, concat_axis=0, tiled=True)
    picked_packed = jnp.take(
        got_packed.reshape(beam_count * slot_cap, window_width, window_width), flat_slot, axis=0
    )
    picked_packed = picked_packed.reshape(user_count, slot_count, window_width, window_width)
    live = jnp.arange(slot_count, dtype=jnp.int32)[None, :] < window_count[:, None]
    packed = jnp.sum(jnp.where(live[:, :, None, None], picked_packed, 0.0), axis=1)[0]
    return finish_user(packed, window_count, grid_index, beams_total)


def solution(mesh):
    placed = (
        P(None, "beam", "grp"),
        P(("beam", "grp")),
        P(("beam", "grp"), None, None),
        P(("beam", "grp"), None),
        P(("beam", "grp"), None),
    )
    return jax.shard_map(
        local, mesh=mesh, in_specs=placed, out_specs=P(("beam", "grp"), None), check_vma=False
    )
```

time: 339 us -> 147 us (0.43)
  other arithmetic: 236 us -> 9.32 us
  waiting for transfers between devices: 30.4 us -> 73.8 us
  matrix products: 17.9 us -> 1.42 us
  Pallas kernels: 0 us -> 14 us
    another operation x40 -> x0, other arithmetic: 184 us -> none  [the longest x24 99.6 us: orthonormal(): lower_factor = jnp.linalg.cholesky(gram_matrix)]
    all_to_all x1, waiting for transfers between devices: 6.04 us -> 51.4 us  [local(): lax.all_to_all(picked, 'beam', split_axis=0, concat_axis=0, tiled=True)]
    mul x1 -> x0, other arithmetic: 23.3 us -> none  [steering(): magnitude * jnp.cos(phase_angle)]
    concatenate x2 -> x0, other arithmetic: 21.2 us -> none  [the longest x1 21.2 us: steering(): jnp.concatenate([magnitude * jnp.cos(phase_angle), magnitude * jnp.sin(ph...]
    pallas_call x0 -> x1, Pallas kernels: none -> 14 us  [finish_user(): pl.pallas_call(functools.partial(finish_kernel, beams_total), out_shape=j...]
    dot_general x19 -> x0, matrix products: 13.9 us -> none  [the longest x1 6.05 us: finish_users(): jnp.einsum('ugc,ucq->ugq', steering_rows, noise_basis, precision=highest,...]
  transfers between devices with their start and end apart: 2 -> 2, of which waited for: 2 -> 2; matrix products, arithmetic and copies ran while one was open for 14% -> 2% of each run, Pallas kernels for 0% -> 0%
where the time goes in v1:
time: 147 us
  waiting for transfers between devices  73.8 us (50%)
  blocking collectives  15.3 us (10%)
  between operations  14.1 us (10%)
  Pallas kernels  14 us (10%)
  starting transfers between devices  11.9 us (8%)
  other arithmetic  9.32 us (6%)
  local copies, waits for them, and re-layouts  6.97 us (5%)
    all_to_all x1, waiting for transfers between devices, local(): lax.all_to_all(picked, 'beam', split_axis=0, concat_axis=0, tiled=True)  51.4 us
    all_gather x1, waiting for transfers between devices, total_of_pieces(): blocks = lax.all_gather(value, axis)  22.4 us
    all_to_all x1, blocking collectives, local(): lax.all_to_all(requests, 'beam', split_axis=0, concat_axis=0, tiled=True)  15.3 us
    pallas_call x1, Pallas kernels, finish_user(): pl.pallas_call(functools.partial(finish_kernel, beams_total), out_shape=j...  14 us
    all_to_all x1, starting transfers between devices, local(): lax.all_to_all(picked, 'beam', split_axis=0, concat_axis=0, tiled=True)  11.9 us
    select_n x2, other arithmetic, local(): jnp.take(window_packed, lax.all_to_all(requests, 'beam', split_axis=0, co...  4.46 us
  transfers between devices with their start and end apart: 2, of which 2 were waited for; matrix products, arithmetic and copies ran while one was open for 2% of the time, Pallas kernels for 0%

profile of v1, /device:TPU:1, one launch (start us, length us, event | category | flops | bytes accessed | tf_op | source)
XLA Modules:
  0.0 147.0 jit_solution(7033952896391050515)
XLA Ops:
  6.5 0.0 all-gather.3.cloned.1.call-start
  6.6 0.8 fusion.9
  7.4 0.2 fusion.5
  7.6 0.2 fusion.1
  7.9 0.1 copy.39
  8.0 1.0 fusion
  9.0 0.0 all-gather.3.cloned.1.call-update
  9.0 0.7 fusion.7
  9.7 0.8 select_reduce_fusion.1
  10.6 0.7 multiply_reduce_fusion
  11.3 0.1 copy.30
  11.4 15.3 %all_to_all.20 = s32[32,1,2]{2,1,0:T(1,128)S(1)} all-to-all(s32[32,1,2]{2,1,0:T(1,128)S(1)} %copy.30), channel_id=1, replica_groups=mesh['beam'=32,'grp'=8] {'beam'}, dimensions={0} | all-to-all | bytes 512 | tf_op jit(solution)/shard_map/all_to_all | solution.py:205
  26.8 0.1 copy.31
  26.8 0.1 copy.41
  26.9 0.1 reshape.159
  27.1 0.1 copy.32
  27.2 22.4 %all-gather.3.cloned.1.call-done = f32[32,128,128]{2,1,0:T(8,128)} async-done(((f32[4,128,128]{2,1,0:T(8,128)}), f32[32,128,128]{2,1,0:T(8,128)}) %all-gather.3.cloned.1.call-update) | async-done | bytes 2097168 | tf_op jit(solution)/shard_map/all_gather | solution.py:23
  49.6 1.7 %reduce_sum.40 = f32[4,128,128]{2,1,0:T(8,128)S(1)} reduce(f32[8,4,128,128]{3,2,1,0:T(8,128)} %bitcast.32, f32[]{:T(128)} %constant.37.clone.1), dimensions={0}, to_apply=%region_3.4 | reduce | flops 458752 | bytes 2359300 | tf_op jit(solution)/shard_map/reduce_sum | solution.py:24
  51.3 2.8 %gather_fusion = f32[64,128,128]{2,1,0:T(8,128)} fusion(f32[4,128,128]{2,1,0:T(8,128)S(1)} %reduce_sum.40, s32[1024]{0:T(1024)S(1)} %pad_clamp_fusion.1), kind=kCustom, calls=%fused_computation | custom fusion | bytes 8388864 | tf_op jit(solution)/shard_map/jit(_take)/gather | solution.py:203
  54.1 4.5 %broadcast_select_fusion = f32[32,2,128,128]{3,2,1,0:T(8,128)} fusion(f32[32,2,128,128]{3,2,1,0:T(8,128)} %bitcast.31, pred[32,2]{1,0:T(8,128)(4,1)S(1)} %copy.32), kind=kLoop, calls=%fused_computation.2 | loop fusion | flops 1048576 | bytes 8388672 | tf_op jit(solution)/shard_map/jit(_take)/select_n | solution.py:203
  58.5 0.0 copy-start
  58.5 11.9 %all-to-all-start.1 = ((f32[32,2,128,128]{3,2,1,0:T(8,128)}), f32[32,2,128,128]{3,2,1,0:T(8,128)}, u32[]{:S(2)}, u32[]{:S(2)}) async-start(f32[32,2,128,128]{3,2,1,0:T(8,128)} %broadcast_select_fusion), calls=%async_computation.1 | async-start | bytes 8388608 | tf_op jit(solution)/shard_map/all_to_all | solution.py:208
  71.1 0.0 copy-done
  71.2 51.4 %all-to-all-done.1 = f32[32,2,128,128]{3,2,1,0:T(8,128)} async-done(((f32[32,2,128,128]{3,2,1,0:T(8,128)}), f32[32,2,128,128]{3,2,1,0:T(8,128)}, u32[]{:S(2)}, u32[]{:S(2)}) %all-to-all-start.1) | async-done | bytes 4194336 | tf_op jit(solution)/shard_map/all_to_all | solution.py:208
  122.6 2.8 %gather_fusion.1 = f32[8,128,128]{2,1,0:T(8,128)S(1)} fusion(f32[64,128,128]{2,1,0:T(8,128)} %bitcast.9, s32[1024]{0:T(1024)S(1)} %pad_clamp_fusion), kind=kCustom, calls=%fused_computation.1 | custom fusion | bytes 1048608 | tf_op jit(solution)/shard_map/jit(_take)/gather | solution.py:209
  125.4 0.7 select_reduce_fusion.packed_ref
  126.1 14.0 %finish_user.1 = f32[1,4096]{1,0:T(1,128)} custom-call(f32[128,128]{1,0:T(8,128)} %select_reduce_fusion.packed_ref, s32[1]{0:T(128)} %copy.50.count_ref, s32[1,4096]{1,0:T(1,128)} %grid_ref.1), custom_call_target="tpu_custom_call" | custom-call | tf_op jit(solution)/shard_map/finish_user/pallas_call | solution.py:172
  (11 shorter events, 0.1 us)
Async XLA Ops:
  6.5 43.0 %all-gather.3.cloned.1.call-start = ((), (), s32[]{:S(2)}) async-start(), calls=%async_computation.2 | async-start | bytes 2359296 | tf_op jit(solution)/shard_map/all_gather | solution.py:23
  58.5 12.6 %copy-start = (s32[1,8,1]{1,2,0:T(1,128)S(1)}, s32[1,8,1]{1,2,0:T(1,128)}, u32[]{:S(2)}) copy-start(s32[1,8,1]{1,2,0:T(1,128)} %param.7) | copy-start | bytes 100
  58.5 64.1 %all-to-all-start.1 = ((f32[32,2,128,128]{3,2,1,0:T(8,128)}), f32[32,2,128,128]{3,2,1,0:T(8,128)}, u32[]{:S(2)}, u32[]{:S(2)}) async-start(f32[32,2,128,128]{3,2,1,0:T(8,128)} %broadcast_select_fusion), calls=%async_computation.1 | async-start | bytes 8388608 | tf_op jit(solution)/shard_map/all_to_all | solution.py:208
Sparse Core Ops, SparseCore 0:
  9.1 40.4 all-gather.2

commit v2 on v1

--- a/solution.py
+++ b/solution.py
@@ -12,49 +12,162 @@
 SNAPS = 256
 OVERSAMPLE = 32
 ITERS = 8
-
-
-highest = lax.Precision.HIGHEST
+SIDE = 4
+MESH = pl.DeviceIdType.MESH
+
 shift_factor = 1.05
 spectral_floor = 0.05
 
 
-def total_of_pieces(value, axis):
-    blocks = lax.all_gather(value, axis)
-    return blocks.sum(axis=0)
-
-
-def owner_slots(owners, locals_flat, beam_count, slot_cap):
-    owner_hits = (owners[:, None] == jnp.arange(beam_count, dtype=jnp.int32)[None, :]).astype(
-        jnp.int32
-    )
-    earlier = jnp.cumsum(owner_hits, axis=0) - owner_hits
-    order_in = jnp.sum(earlier * owner_hits, axis=1)
-    slot_match = owner_hits[:, :, None] * (
-        order_in[:, None, None] == jnp.arange(slot_cap, dtype=jnp.int32)[None, None, :]
-    ).astype(jnp.int32)
-    requests = jnp.sum(slot_match * locals_flat[:, None, None], axis=0)
-    return (requests, owners * slot_cap + order_in)
-
-
-def pack_upper(same_part, imag_part):
-    width = same_part.shape[-1]
-    row_ids = jnp.arange(width, dtype=jnp.int32)[:, None]
-    col_ids = jnp.arange(width, dtype=jnp.int32)[None, :]
-    return jnp.where((row_ids <= col_ids)[None], same_part, imag_part)
-
-
-def local_grams(window_view):
-    same_part = jnp.einsum(
-        "wis,wjs->wij", window_view[0], window_view[0], preferred_element_type=jnp.float32
-    )
-    same_part = same_part + jnp.einsum(
-        "wis,wjs->wij", window_view[1], window_view[1], preferred_element_type=jnp.float32
-    )
-    cross_part = jnp.einsum(
-        "wis,wjs->wij", window_view[1], window_view[0], preferred_element_type=jnp.float32
-    )
-    return (same_part, cross_part)
+def remote(source, target, send_sem, recv_sem, device):
+    return pltpu.make_async_remote_copy(
+        src_ref=source,
+        dst_ref=target,
+        send_sem=send_sem,
+        recv_sem=recv_sem,
+        device_id=device,
+        device_id_type=MESH,
+    )
+
+
+def dot_tn(left, right):
+    return lax.dot_general(
+        left, right, (((0,), (0,)), ((), ())), preferred_element_type=jnp.float32
+    )
+
+
+def exchange_kernel(
+    groups, slots, x_ref, meta_ref, out_ref, raw, metas, chosen, blocks, sums, parts,
+    raw_send, raw_recv, meta_send, meta_recv, block_send, block_recv, part_send, part_recv, local_sem,
+):
+    b, g = lax.axis_index("beam"), lax.axis_index("grp")
+    core, x, y = b % 2, b // (2 * SIDE), (b // 2) % SIDE
+    rows = WIN_BEAMS // 2
+
+    def along(first, second):
+        at_x = (x + first * (1 - core) + second * core) % SIDE
+        at_y = (y + first * core + second * (1 - core)) % SIDE
+        return (at_x * SIDE + at_y) * 2 + core
+
+    partner = b + 1 - 2 * core
+    line = [(g + d) % groups for d in range(groups)]
+    barrier = pltpu.get_barrier_semaphore()
+    greeted = [(b, line[d]) for d in range(1, groups)]
+    greeted += [(along(d, 0), g) for d in range(1, SIDE)] + [(along(0, d), g) for d in range(1, SIDE)]
+    greeted += [(partner, g)]
+    for device in greeted:
+        pl.semaphore_signal(barrier, inc=1, device_id=device, device_id_type=MESH)
+    pl.semaphore_wait(barrier, len(greeted))
+
+    sent = []
+
+    def send(*args):
+        copy = remote(*args)
+        copy.start()
+        sent.append(copy)
+
+    for d in range(1, groups):
+        send(x_ref.at[line[d] // 2], raw.at[g], raw_send.at[d], raw_recv.at[g], (b, line[d]))
+    for d in range(1, groups):
+        send(meta_ref, metas.at[g], meta_send.at[d], meta_recv.at[g], (b, line[d]))
+    raw[g] = x_ref[g // 2]
+    metas[g] = meta_ref[...]
+    for d in range(1, groups):
+        remote(x_ref.at[0], raw.at[line[d]], raw_send.at[d], raw_recv.at[line[d]], (b, line[d])).wait_recv()
+    real = raw[:, 0].reshape(SNAPS, WIN_BEAMS)
+    imag = raw[:, 1].reshape(SNAPS, WIN_BEAMS)
+    same = dot_tn(real, real) + dot_tn(imag, imag)
+    cross = dot_tn(imag, real) - dot_tn(real, imag)
+    row = lax.broadcasted_iota(jnp.int32, (WIN_BEAMS, WIN_BEAMS), 0)
+    col = lax.broadcasted_iota(jnp.int32, (WIN_BEAMS, WIN_BEAMS), 1)
+    packed = jnp.where(row <= col, same, cross)
+    blocks[b] = jnp.where(g % 2 == 0, packed[:rows], packed[rows:])
+
+    count = [0]
+
+    def pass_on(block, device):
+        send(blocks.at[block], blocks.at[block], block_send.at[count[0]], block_recv.at[block], (device, g))
+        count[0] += 1
+
+    def arrived(block):
+        remote(blocks.at[block], blocks.at[block], block_send.at[0], block_recv.at[block], (partner, g)).wait_recv()
+
+    for d in (1, 3, 2):
+        pass_on(b, along(d, 0))
+    for d in (1, 3, 2):
+        pass_on(b, along(0, d))
+    pass_on(b, partner)
+    for d in range(1, groups):
+        remote(meta_ref, metas.at[line[d]], meta_send.at[d], meta_recv.at[line[d]], (b, line[d])).wait_recv()
+    fetch = pltpu.make_async_copy(metas, chosen, local_sem)
+    fetch.start()
+    for e in (1, 3, 2):
+        block = along(e, 0)
+        arrived(block)
+        for d in (1, 3, 2):
+            pass_on(block, along(0, d))
+        pass_on(block, partner)
+    for e in (0, 1, 3, 2):
+        for d in (1, 3, 2):
+            block = along(e, d)
+            arrived(block)
+            pass_on(block, partner)
+    fetch.wait()
+    for i in range(SIDE * SIDE):
+        arrived(2 * i + 1 - core)
+
+    for d in list(range(1, groups)) + [0]:
+        user = line[d]
+        total = jnp.zeros((rows, WIN_BEAMS), jnp.float32)
+        for k in range(slots):
+            weight = jnp.where(chosen[user, 0, slots + k] == g // 2, 1.0, 0.0)
+            total = total + weight * blocks[chosen[user, 0, k]]
+        if d == 0:
+            parts[g] = total
+        else:
+            sums[d] = total
+            send(sums.at[d], parts.at[g], part_send.at[d], part_recv.at[g], (b, user))
+    for d in range(1, groups):
+        remote(sums.at[d], parts.at[line[d]], part_send.at[d], part_recv.at[line[d]], (b, line[d])).wait_recv()
+    for h in range(2):
+        total = parts[h]
+        for w in range(1, groups // 2):
+            total = total + parts[2 * w + h]
+        out_ref[h * rows : (h + 1) * rows, :] = total
+    for copy in sent:
+        copy.wait_send()
+
+
+def exchange(x, meta, groups, owners, slots):
+    rows = WIN_BEAMS // 2
+    vmem = pl.BlockSpec(memory_space=pltpu.VMEM)
+    dma = pltpu.SemaphoreType.DMA
+    forwards = 2 * (SIDE - 1) + 1 + (SIDE - 1) * SIDE + SIDE * (SIDE - 1)
+    return pl.pallas_call(
+        functools.partial(exchange_kernel, groups, slots),
+        out_shape=jax.ShapeDtypeStruct((WIN_BEAMS, WIN_BEAMS), jnp.float32),
+        in_specs=[vmem, vmem],
+        out_specs=vmem,
+        scratch_shapes=[
+            pltpu.VMEM((groups,) + x.shape[1:], x.dtype),
+            pltpu.VMEM((groups,) + meta.shape, meta.dtype),
+            pltpu.SMEM((groups,) + meta.shape, meta.dtype),
+            pltpu.VMEM((owners, rows, WIN_BEAMS), jnp.float32),
+            pltpu.VMEM((groups, rows, WIN_BEAMS), jnp.float32),
+            pltpu.VMEM((groups, rows, WIN_BEAMS), jnp.float32),
+            dma((groups,)),
+            dma((groups,)),
+            dma((groups,)),
+            dma((groups,)),
+            dma((forwards,)),
+            dma((owners,)),
+            dma((groups,)),
+            dma((groups,)),
+            dma,
+        ],
+        compiler_params=pltpu.CompilerParams(collective_id=0, has_side_effects=True),
+        name="exchange",
+    )(x, meta)
 
 
 GROW = (3.4445, -4.7750, 2.0315)
@@ -184,35 +297,15 @@
 
 
 def local(beam_data, window_count, slot_owner, slot_window, grid_index):
-    beam_count = lax.axis_size("beam")
-    user_count = window_count.shape[0]
-    slot_count = slot_window.shape[1]
-    window_width = WIN_BEAMS
-    local_windows = beam_data.shape[1] // window_width
-    slot_cap = (user_count * slot_count + beam_count - 1) // beam_count + 1
-    beams_total = beam_data.shape[1] * beam_count
-    snap_local = beam_data.shape[2]
-    owners = slot_owner[:, :, 0]
-    window_view = beam_data.reshape(2, local_windows, window_width, snap_local)
-    same_part, cross_part = local_grams(window_view)
-    packed_part = pack_upper(same_part, cross_part - jnp.swapaxes(cross_part, 1, 2))
-    window_packed = total_of_pieces(packed_part, "grp")
-    requests, flat_slot = owner_slots(
-        owners.reshape(-1), slot_window.reshape(-1), beam_count, slot_cap
-    )
-    picked = jnp.take(
-        window_packed,
-        lax.all_to_all(requests, "beam", split_axis=0, concat_axis=0, tiled=True),
-        axis=0,
-    )
-    got_packed = lax.all_to_all(picked, "beam", split_axis=0, concat_axis=0, tiled=True)
-    picked_packed = jnp.take(
-        got_packed.reshape(beam_count * slot_cap, window_width, window_width), flat_slot, axis=0
-    )
-    picked_packed = picked_packed.reshape(user_count, slot_count, window_width, window_width)
-    live = jnp.arange(slot_count, dtype=jnp.int32)[None, :] < window_count[:, None]
-    packed = jnp.sum(jnp.where(live[:, :, None, None], picked_packed, 0.0), axis=1)[0]
-    return finish_user(packed, window_count, grid_index, beams_total)
+    owners, groups = lax.axis_size("beam"), lax.axis_size("grp")
+    slots = slot_window.shape[1]
+    windows = beam_data.shape[1] // WIN_BEAMS
+    x = beam_data.reshape(2, windows, WIN_BEAMS, beam_data.shape[2]).transpose(1, 0, 3, 2)
+    live = jnp.arange(slots, dtype=jnp.int32)[None, :] < window_count[:, None]
+    words = jnp.concatenate([slot_owner[:, :, 0], jnp.where(live, slot_window, -1)], axis=1)
+    meta = jnp.broadcast_to(jnp.pad(words, ((0, 0), (0, 128 - 2 * slots))), (8, 128))
+    packed = exchange(x, meta, groups, owners, slots)
+    return finish_user(packed, window_count, grid_index, beam_data.shape[1] * owners)
 
 
 def solution(mesh):

time: 147 us -> 56.1 us (0.38)
  waiting for transfers between devices: 73.8 us -> 0 us
  Pallas kernels: 14 us -> 52.5 us
  blocking collectives: 15.3 us -> 0 us
  between operations: 14.1 us -> 0.71 us
  starting transfers between devices: 11.9 us -> 0 us
  other arithmetic: 9.32 us -> 0.08 us
  local copies, waits for them, and re-layouts: 6.97 us -> 2.55 us
    all_to_all x1 -> x0, waiting for transfers between devices: 51.4 us -> none  [local(): lax.all_to_all(picked, 'beam', split_axis=0, concat_axis=0, tiled=True)]
    pallas_call x0 -> x1, Pallas kernels: none -> 38.5 us  [exchange(): pl.pallas_call(functools.partial(exchange_kernel, groups, slots), out_sha...]
    all_gather x1 -> x0, waiting for transfers between devices: 22.4 us -> none  [total_of_pieces(): blocks = lax.all_gather(value, axis)]
    all_to_all x1 -> x0, blocking collectives: 15.3 us -> none  [local(): lax.all_to_all(requests, 'beam', split_axis=0, concat_axis=0, tiled=True)]
    all_to_all x1 -> x0, starting transfers between devices: 11.9 us -> none  [local(): lax.all_to_all(picked, 'beam', split_axis=0, concat_axis=0, tiled=True)]
    gather x2 -> x0, local copies, waits for them, and re-layouts: 5.55 us -> none  [the longest x1 2.79 us: local(): jnp.take(window_packed, lax.all_to_all(requests, 'beam', split_axis=0, co...]
    select_n x3 -> x1, other arithmetic: 4.47 us -> 0.01 us  [local(): jnp.where(live, slot_window, -1)]
    reduce_sum x4 -> x0, other arithmetic: 4.04 us -> none  [the longest x1 1.72 us: total_of_pieces(): return blocks.sum(axis=0)]
  transfers between devices with their start and end apart: 2 -> 0, of which waited for: 2 -> 0; matrix products, arithmetic and copies ran while one was open for 2% -> 0% of each run, Pallas kernels for 0% -> 0%
where the time goes in v2:
time: 56.1 us; the launch traced here: 55.8 us
  Pallas kernels  52.5 us (94%)
  local copies, waits for them, and re-layouts  2.55 us (5%)
  between operations  0.71 us (1%)
    pallas_call x1, Pallas kernels, exchange(): pl.pallas_call(functools.partial(exchange_kernel, groups, slots), out_sha...  38.5 us
    pallas_call x1, Pallas kernels, finish_user(): pl.pallas_call(functools.partial(finish_kernel, beams_total), out_shape=j...  14 us
    unnamed x6, local copies, waits for them, and re-layouts  1.3 us

profile of v2, /device:TPU:1, one launch (start us, length us, event | category | flops | bytes accessed | tf_op | source)
XLA Modules:
  0.0 55.8 jit_solution(9974566442532268381)
XLA Ops:
  0.0 0.0 copy-start
  0.7 0.0 copy-start.1
  0.7 0.6 %copy-done.1 = s32[1,8]{1,0:T(1,128)S(1)} copy-done((s32[1,8]{1,0:T(1,128)S(1)}, s32[1,8]{1,0:T(1,128)}, u32[]{:S(2)}) %copy-start.1) | copy-done | bytes 56
  1.3 0.0 copy-start.2
  1.4 0.6 %copy-done.2 = s32[1,8,1]{1,2,0:T(1,128)S(1)} copy-done((s32[1,8,1]{1,2,0:T(1,128)S(1)}, s32[1,8,1]{1,2,0:T(1,128)}, u32[]{:S(2)}) %copy-start.2) | copy-done | bytes 56
  2.0 0.1 pad_add_fusion
  2.1 0.6 %broadcast_in_dim.15.meta_ref = s32[8,128]{1,0:T(8,128)} broadcast(s32[128]{0:T(128)S(1)} %pad_bitcast_fusion), dimensions={1} | broadcast | bytes 4608 | tf_op jit(solution)/shard_map/broadcast_in_dim | solution.py:306
  2.7 0.0 copy-done
  2.7 0.6 %bitcast_bitcast_fusion.x_ref = bf16[4,2,32,128]{3,2,1,0:T(8,128)(2,1)} fusion(bf16[2,512,32]{1,2,0:T(8,128)(2,1)S(1)} %copy-done), kind=kLoop, calls=%fused_computation | loop fusion | bytes 131072 | tf_op jit(solution)/shard_map/transpose | solution.py:303
  3.3 38.5 %exchange.1.packed_ref = f32[128,128]{1,0:T(8,128)} custom-call(bf16[4,2,32,128]{3,2,1,0:T(8,128)(2,1)} %bitcast_bitcast_fusion.x_ref, s32[8,128]{1,0:T(8,128)} %broadcast_in_dim.15.meta_ref), custom_call_target="tpu_custom_call" | custom-call | tf_op jit(solution)/shard_map/exchange/pallas_call | solution.py:146
  41.8 14.0 %finish_user.1 = f32[1,4096]{1,0:T(1,128)} custom-call(f32[128,128]{1,0:T(8,128)} %exchange.1.packed_ref, s32[1]{0:T(128)} %copy.9.count_ref, s32[1,4096]{1,0:T(1,128)} %grid_ref.1), custom_call_target="tpu_custom_call" | custom-call | tf_op jit(solution)/shard_map/finish_user/pallas_call | solution.py:285
  (2 shorter events, 0.0 us)
Async XLA Ops:
  0.0 2.7 %copy-start = (bf16[2,512,32]{1,2,0:T(8,128)(2,1)S(1)}, bf16[2,512,32]{1,2,0:T(8,128)(2,1)}, u32[]{:S(2)}) copy-start(bf16[2,512,32]{1,2,0:T(8,128)(2,1)} %param.5) | copy-start | bytes 196612
  0.7 0.7 %copy-start.1 = (s32[1,8]{1,0:T(1,128)S(1)}, s32[1,8]{1,0:T(1,128)}, u32[]{:S(2)}) copy-start(s32[1,8]{1,0:T(1,128)} %param.8) | copy-start | bytes 100
  1.3 0.7 %copy-start.2 = (s32[1,8,1]{1,2,0:T(1,128)S(1)}, s32[1,8,1]{1,2,0:T(1,128)}, u32[]{:S(2)}) copy-start(s32[1,8,1]{1,2,0:T(1,128)} %param.7) | copy-start | bytes 100

commit v3 on v2

--- a/solution.py
+++ b/solution.py
@@ -37,7 +37,7 @@
 
 
 def exchange_kernel(
-    groups, slots, x_ref, meta_ref, out_ref, raw, metas, chosen, blocks, sums, parts,
+    groups, slots, x_ref, count_ref, owner_ref, window_ref, out_ref, meta_ref, raw, metas, chosen, blocks, sums, parts,
     raw_send, raw_recv, meta_send, meta_recv, block_send, block_recv, part_send, part_recv, local_sem,
 ):
     b, g = lax.axis_index("beam"), lax.axis_index("grp")
@@ -48,6 +48,9 @@
         at_x = (x + first * (1 - core) + second * core) % SIDE
         at_y = (y + first * core + second * (1 - core)) % SIDE
         return (at_x * SIDE + at_y) * 2 + core
+
+    def window_of(w):
+        return x_ref.at[:, :, pl.ds(pl.multiple_of(w * WIN_BEAMS, WIN_BEAMS), WIN_BEAMS)]
 
     partner = b + 1 - 2 * core
     line = [(g + d) % groups for d in range(groups)]
@@ -55,6 +58,12 @@
     greeted = [(b, line[d]) for d in range(1, groups)]
     greeted += [(along(d, 0), g) for d in range(1, SIDE)] + [(along(0, d), g) for d in range(1, SIDE)]
     greeted += [(partner, g)]
+    lane = lax.broadcasted_iota(jnp.int32, meta_ref.shape, 1)
+    meta = jnp.full(meta_ref.shape, -1, jnp.int32)
+    for k in range(slots):
+        wanted = jnp.where(k < count_ref[0], window_ref[0, k], -1)
+        meta = jnp.where(lane == k, owner_ref[0, k], jnp.where(lane == slots + k, wanted, meta))
+    meta_ref[...] = meta
     for device in greeted:
         pl.semaphore_signal(barrier, inc=1, device_id=device, device_id_type=MESH)
     pl.semaphore_wait(barrier, len(greeted))
@@ -67,13 +76,13 @@
         sent.append(copy)
 
     for d in range(1, groups):
-        send(x_ref.at[line[d] // 2], raw.at[g], raw_send.at[d], raw_recv.at[g], (b, line[d]))
+        send(window_of(line[d] // 2), raw.at[g], raw_send.at[d], raw_recv.at[g], (b, line[d]))
     for d in range(1, groups):
         send(meta_ref, metas.at[g], meta_send.at[d], meta_recv.at[g], (b, line[d]))
-    raw[g] = x_ref[g // 2]
+    raw[g] = window_of(g // 2)[...]
     metas[g] = meta_ref[...]
     for d in range(1, groups):
-        remote(x_ref.at[0], raw.at[line[d]], raw_send.at[d], raw_recv.at[line[d]], (b, line[d])).wait_recv()
+        remote(window_of(0), raw.at[line[d]], raw_send.at[d], raw_recv.at[line[d]], (b, line[d])).wait_recv()
     real = raw[:, 0].reshape(SNAPS, WIN_BEAMS)
     imag = raw[:, 1].reshape(SNAPS, WIN_BEAMS)
     same = dot_tn(real, real) + dot_tn(imag, imag)
@@ -138,20 +147,22 @@
         copy.wait_send()
 
 
-def exchange(x, meta, groups, owners, slots):
+def exchange(x, count, owner, window, groups, owners, slots):
     rows = WIN_BEAMS // 2
-    vmem = pl.BlockSpec(memory_space=pltpu.VMEM)
+    vmem, smem = pl.BlockSpec(memory_space=pltpu.VMEM), pl.BlockSpec(memory_space=pltpu.SMEM)
+    meta = (8, 128)
     dma = pltpu.SemaphoreType.DMA
     forwards = 2 * (SIDE - 1) + 1 + (SIDE - 1) * SIDE + SIDE * (SIDE - 1)
     return pl.pallas_call(
         functools.partial(exchange_kernel, groups, slots),
         out_shape=jax.ShapeDtypeStruct((WIN_BEAMS, WIN_BEAMS), jnp.float32),
-        in_specs=[vmem, vmem],
+        in_specs=[vmem, smem, smem, smem],
         out_specs=vmem,
         scratch_shapes=[
-            pltpu.VMEM((groups,) + x.shape[1:], x.dtype),
-            pltpu.VMEM((groups,) + meta.shape, meta.dtype),
-            pltpu.SMEM((groups,) + meta.shape, meta.dtype),
+            pltpu.VMEM(meta, jnp.int32),
+            pltpu.VMEM((groups,) + x.shape[:2] + (WIN_BEAMS,), x.dtype),
+            pltpu.VMEM((groups,) + meta, jnp.int32),
+            pltpu.SMEM((groups,) + meta, jnp.int32),
             pltpu.VMEM((owners, rows, WIN_BEAMS), jnp.float32),
             pltpu.VMEM((groups, rows, WIN_BEAMS), jnp.float32),
             pltpu.VMEM((groups, rows, WIN_BEAMS), jnp.float32),
@@ -167,13 +178,15 @@
         ],
         compiler_params=pltpu.CompilerParams(collective_id=0, has_side_effects=True),
         name="exchange",
-    )(x, meta)
+    )(x, count, owner, window)
 
 
 GROW = (3.4445, -4.7750, 2.0315)
-CLOSE = ((3.109266, -3.792034, 1.535381), (1.90467, -1.282586, 0.3782733), (1.875, -1.25, 0.375))
-EXTRA = 6
-CHUNK = 512
+CLOSE = ((3.109266, -3.792034, 1.535381), (1.90467, -1.282586, 0.3782733))
+LAST = (1.875, -1.25, 0.375)
+NEAR = 0.012
+ROUNDS = 8
+PIECES = 8
 
 
 def halves(value):
@@ -208,8 +221,12 @@
     return jnp.concatenate([top, jnp.concatenate([-top[:, n:], top[:, :n]], axis=1)], axis=0)
 
 
-def finish_kernel(beams_total, packed_ref, count_ref, grid_ref, out_ref, a_hi, a_lo, w_ref):
+def finish_kernel(
+    beams_total, packed_ref, count_ref, grid_ref, out_ref, a_hi, a_lo, w_ref, gram_ref, c_hi, c_lo, length_ref
+):
     n = WIN_BEAMS
+    chunk = grid_ref.shape[1] // PIECES
+    slope = jnp.pi / beams_total
     row = lax.broadcasted_iota(jnp.int32, (n, n), 0)
     col = lax.broadcasted_iota(jnp.int32, (n, n), 1)
     packed = packed_ref[...]
@@ -231,56 +248,69 @@
     w_ref[...] = jnp.concatenate([shifted[:NOISE_DIM], shifted[n : n + NOISE_DIM]], axis=0)
     eye = jnp.where(row == col, 1.0, 0.0)
 
-    def step(coefs, apply_a, precise):
+    def steer(piece):
+        where = pl.ds(pl.multiple_of(piece * chunk, chunk), chunk)
+        position = (grid_ref[:, where].astype(jnp.float32) + 0.5) / OVERSAMPLE
+        offset = position - lax.broadcasted_iota(jnp.int32, (n, chunk), 0).astype(jnp.float32)
+        angle = (slope * offset) * (slope * offset)
+        series = 1.0 / 3.0 + angle * (1.0 / 45.0 + angle * (2.0 / 945.0))
+        cot = 1.0 / offset - (slope * slope * offset) * series
+        high, low = halves(cot)
+        c_hi[:, where] = high
+        c_lo[:, where] = low
+        length_ref[:, where] = jnp.sum(cot * cot, axis=0, keepdims=True) + n * slope * slope
+
+    def step(coefs, apply_a=False):
         a, b, c = coefs
-        basis = w_ref[...]
-        parts = halves(basis)
+        parts = halves(w_ref[...])
         gram = dot_nt(parts[0], parts[0])
-        if precise:
-            gram = gram + (dot_nt(parts[0], parts[1]) + dot_nt(parts[1], parts[0]))
-            gram_parts = halves(gram)
-            gram2 = product_half(gram_parts, gram_parts)
-        else:
-            low = gram.astype(jnp.bfloat16)
-            gram2 = dot(low, low)
-        if apply_a:
-            moved = halves(product(parts, (a_hi[...], a_lo[...])))
-        else:
-            moved = parts
-        mix = halves(a * eye + b * gram + c * gram2)
-        w_ref[...] = product_half(mix, moved)
+        low = gram.astype(jnp.bfloat16)
+        mix = a * eye + b * gram + c * dot(low, low)
+        moved = halves(product(parts, (a_hi[...], a_lo[...]))) if apply_a else parts
+        w_ref[...] = product_half(halves(mix), moved)
+
+    def distance():
+        parts = halves(w_ref[...])
+        cross = dot_nt(parts[0], parts[1])
+        gram = dot_nt(parts[0], parts[0]) + (cross + dot_nt(parts[1], parts[0]))
+        gram_ref[...] = gram
+        return jnp.sum((gram - eye) * (gram - eye))
 
     @pl.loop(0, ITERS - 1)
-    def _(_):
-        step(GROW, True, False)
-
-    @pl.loop(0, EXTRA)
-    def _(_):
-        step(GROW, False, False)
-
-    step(CLOSE[0], False, False)
-    step(CLOSE[1], False, False)
-    step(CLOSE[2], False, True)
-    basis = w_ref[...]
-    slope = jnp.pi / beams_total
+    def _(i):
+        step(GROW, True)
+        steer(i)
+
+    step(CLOSE[0])
+    steer(ITERS - 1)
+    step(CLOSE[1])
+
+    def again(state):
+        step(GROW)
+        step(GROW)
+        step(CLOSE[0])
+        step(CLOSE[1])
+        return state[0] + 1, distance()
+
+    lax.while_loop(
+        lambda state: (state[1] > NEAR) & (state[0] < ROUNDS), again, (jnp.int32(0), distance())
+    )
+    gram = gram_ref[...]
+    parts = halves(gram)
+    mix = LAST[0] * eye + LAST[1] * gram + LAST[2] * product_half(parts, parts)
+    basis = product_half(halves(mix), halves(w_ref[...]))
     bias = -slope * jnp.sum(basis[:, n:], axis=1, keepdims=True)
     lead = halves(basis[:, :n])
-
-    @pl.loop(0, grid_ref.shape[1] // CHUNK)
-    def _(i):
-        where = pl.ds(pl.multiple_of(i * CHUNK, CHUNK), CHUNK)
-        position = (grid_ref[:, where].astype(jnp.float32) + 0.5) / OVERSAMPLE
-        offset = position - lax.broadcasted_iota(jnp.int32, (n, CHUNK), 0).astype(jnp.float32)
-        angle = (slope * offset) * (slope * offset)
-        cot = 1.0 / offset - (slope * slope * offset) * (1.0 / 3.0 + angle * (1.0 / 45.0 + angle * (2.0 / 945.0)))
-        projected = product_half(lead, halves(cot)) + bias
+    for piece in range(PIECES):
+        where = slice(piece * chunk, (piece + 1) * chunk)
+        projected = product_half(lead, (c_hi[:, where], c_lo[:, where])) + bias
         energy = jnp.sum(projected * projected, axis=0, keepdims=True)
-        length = jnp.sum(cot * cot, axis=0, keepdims=True) + n * slope * slope
-        out_ref[:, where] = 1.0 / (energy / length + spectral_floor)
+        out_ref[:, where] = 1.0 / (energy / length_ref[:, where] + spectral_floor)
 
 
 def finish_user(packed, count, grid_index, beams_total):
     n = WIN_BEAMS
+    points = grid_index.shape[1]
     vmem = pl.BlockSpec(memory_space=pltpu.VMEM)
     return pl.pallas_call(
         functools.partial(finish_kernel, beams_total),
@@ -291,6 +321,10 @@
             pltpu.VMEM((2 * n, 2 * n), jnp.bfloat16),
             pltpu.VMEM((2 * n, 2 * n), jnp.bfloat16),
             pltpu.VMEM((n, 2 * n), jnp.float32),
+            pltpu.VMEM((n, n), jnp.float32),
+            pltpu.VMEM((n, points), jnp.bfloat16),
+            pltpu.VMEM((n, points), jnp.bfloat16),
+            pltpu.VMEM((1, points), jnp.float32),
         ],
         name="finish_user",
     )(packed, count, grid_index)
@@ -299,12 +333,8 @@
 def local(beam_data, window_count, slot_owner, slot_window, grid_index):
     owners, groups = lax.axis_size("beam"), lax.axis_size("grp")
     slots = slot_window.shape[1]
-    windows = beam_data.shape[1] // WIN_BEAMS
-    x = beam_data.reshape(2, windows, WIN_BEAMS, beam_data.shape[2]).transpose(1, 0, 3, 2)
-    live = jnp.arange(slots, dtype=jnp.int32)[None, :] < window_count[:, None]
-    words = jnp.concatenate([slot_owner[:, :, 0], jnp.where(live, slot_window, -1)], axis=1)
-    meta = jnp.broadcast_to(jnp.pad(words, ((0, 0), (0, 128 - 2 * slots))), (8, 128))
-    packed = exchange(x, meta, groups, owners, slots)
+    x = beam_data.transpose(0, 2, 1)
+    packed = exchange(x, window_count, slot_owner[:, :, 0], slot_window, groups, owners, slots)
     return finish_user(packed, window_count, grid_index, beam_data.shape[1] * owners)
 
 

time: 56.1 us -> 49.3 us (0.88)
  Pallas kernels: 52.5 us -> 48.5 us
  local copies, waits for them, and re-layouts: 2.55 us -> 0 us
    pallas_call x1, Pallas kernels: 14 us -> 9.81 us  [finish_user(): pl.pallas_call(functools.partial(finish_kernel, beams_total), out_shape=j...]
    unnamed x6 -> x0, local copies, waits for them, and re-layouts: 1.3 us -> none
    transpose x1 -> x0, local copies, waits for them, and re-layouts: 0.64 us -> none  [local(): beam_data.reshape(2, windows, WIN_BEAMS, beam_data.shape[2])]
    broadcast_in_dim x2 -> x0, local copies, waits for them, and re-layouts: 0.6 us -> none  [local(): jnp.broadcast_to(jnp.pad(words, ((0, 0), (0, 128 - 2 * slots))), (8, 128))]
where the time goes in v3:
time: 49.3 us; the launch traced here: 49.2 us
  Pallas kernels  48.5 us (98%)
  between operations  0.66 us (1%)
    pallas_call x1, Pallas kernels, exchange(): pl.pallas_call(functools.partial(exchange_kernel, groups, slots), out_sha...  38.7 us
    pallas_call x1, Pallas kernels, finish_user(): pl.pallas_call(functools.partial(finish_kernel, beams_total), out_shape=j...  9.81 us

profile of v3, /device:TPU:1, one launch (start us, length us, event | category | flops | bytes accessed | tf_op | source)
XLA Modules:
  0.0 49.2 jit_solution(15049022158437642022)
XLA Ops:
  0.7 38.7 %exchange.1.packed_ref = f32[128,128]{1,0:T(8,128)} custom-call(bf16[2,32,512]{2,1,0:T(8,128)(2,1)} %bitcast.2, s32[1]{0:T(128)S(6)} %copy.6.count_ref, s32[1,8]{1,0:T(1,128)} %bitcast.3, s32[1,8]{1,0:T(1,128)} %window_ref.1), custom_call_target="tpu_custom_call" | custom-call | tf_op jit(solution)/shard_map/exchange/pallas_call | solution.py:156
  39.4 9.8 %finish_user.1 = f32[1,4096]{1,0:T(1,128)} custom-call(f32[128,128]{1,0:T(8,128)} %exchange.1.packed_ref, s32[1]{0:T(128)S(6)} %copy.6.count_ref, s32[1,4096]{1,0:T(1,128)} %grid_ref.1), custom_call_target="tpu_custom_call" | custom-call | tf_op jit(solution)/shard_map/finish_user/pallas_call | solution.py:315

commit v4 on v3

--- a/solution.py
+++ b/solution.py
@@ -37,35 +37,44 @@
 
 
 def exchange_kernel(
-    groups, slots, x_ref, count_ref, owner_ref, window_ref, out_ref, meta_ref, raw, metas, chosen, blocks, sums, parts,
-    raw_send, raw_recv, meta_send, meta_recv, block_send, block_recv, part_send, part_recv, local_sem,
+    groups, slots, x_ref, count_ref, owner_ref, window_ref, out_ref, meta_ref, partial, pieces, metas, chosen, blocks,
+    ready, sums, piece_send, piece_recv, meta_send, meta_recv, block_send, block_recv, sum_send, sum_recv, local_sem,
 ):
     b, g = lax.axis_index("beam"), lax.axis_index("grp")
     core, x, y = b % 2, b // (2 * SIDE), (b // 2) % SIDE
-    rows = WIN_BEAMS // 2
+    windows, rows = blocks.shape[1:3]
 
     def along(first, second):
         at_x = (x + first * (1 - core) + second * core) % SIDE
         at_y = (y + first * core + second * (1 - core)) % SIDE
         return (at_x * SIDE + at_y) * 2 + core
 
-    def window_of(w):
-        return x_ref.at[:, :, pl.ds(pl.multiple_of(w * WIN_BEAMS, WIN_BEAMS), WIN_BEAMS)]
-
     partner = b + 1 - 2 * core
     line = [(g + d) % groups for d in range(groups)]
+    order = sorted(range(1, groups), key=lambda d: -min(d, groups - d))
     barrier = pltpu.get_barrier_semaphore()
-    greeted = [(b, line[d]) for d in range(1, groups)]
+    greeted = [(b, line[d]) for d in order]
     greeted += [(along(d, 0), g) for d in range(1, SIDE)] + [(along(0, d), g) for d in range(1, SIDE)]
     greeted += [(partner, g)]
+    for device in greeted:
+        pl.semaphore_signal(barrier, inc=1, device_id=device, device_id_type=MESH)
+
     lane = lax.broadcasted_iota(jnp.int32, meta_ref.shape, 1)
     meta = jnp.full(meta_ref.shape, -1, jnp.int32)
     for k in range(slots):
         wanted = jnp.where(k < count_ref[0], window_ref[0, k], -1)
         meta = jnp.where(lane == k, owner_ref[0, k], jnp.where(lane == slots + k, wanted, meta))
     meta_ref[...] = meta
-    for device in greeted:
-        pl.semaphore_signal(barrier, inc=1, device_id=device, device_id_type=MESH)
+    row = lax.broadcasted_iota(jnp.int32, (WIN_BEAMS, WIN_BEAMS), 0)
+    col = lax.broadcasted_iota(jnp.int32, (WIN_BEAMS, WIN_BEAMS), 1)
+    for w in range(windows):
+        real = x_ref[0, :, w * WIN_BEAMS : (w + 1) * WIN_BEAMS]
+        imag = x_ref[1, :, w * WIN_BEAMS : (w + 1) * WIN_BEAMS]
+        same = dot_tn(real, real) + dot_tn(imag, imag)
+        cross = dot_tn(imag, real) - dot_tn(real, imag)
+        packed = jnp.where(row <= col, same, cross)
+        for s in range(groups):
+            partial[s, w] = packed[s * rows : (s + 1) * rows]
     pl.semaphore_wait(barrier, len(greeted))
 
     sent = []
@@ -75,35 +84,32 @@
         copy.start()
         sent.append(copy)
 
-    for d in range(1, groups):
-        send(window_of(line[d] // 2), raw.at[g], raw_send.at[d], raw_recv.at[g], (b, line[d]))
-    for d in range(1, groups):
+    for d in order:
+        send(partial.at[line[d]], pieces.at[g], piece_send.at[d], piece_recv.at[g], (b, line[d]))
+    for d in order:
         send(meta_ref, metas.at[g], meta_send.at[d], meta_recv.at[g], (b, line[d]))
-    raw[g] = window_of(g // 2)[...]
     metas[g] = meta_ref[...]
-    for d in range(1, groups):
-        remote(window_of(0), raw.at[line[d]], raw_send.at[d], raw_recv.at[line[d]], (b, line[d])).wait_recv()
-    real = raw[:, 0].reshape(SNAPS, WIN_BEAMS)
-    imag = raw[:, 1].reshape(SNAPS, WIN_BEAMS)
-    same = dot_tn(real, real) + dot_tn(imag, imag)
-    cross = dot_tn(imag, real) - dot_tn(real, imag)
-    row = lax.broadcasted_iota(jnp.int32, (WIN_BEAMS, WIN_BEAMS), 0)
-    col = lax.broadcasted_iota(jnp.int32, (WIN_BEAMS, WIN_BEAMS), 1)
-    packed = jnp.where(row <= col, same, cross)
-    blocks[b] = jnp.where(g % 2 == 0, packed[:rows], packed[rows:])
+    own = partial[g]
+    for d in reversed(order):
+        piece = pieces.at[line[d]]
+        remote(piece, piece, piece_send.at[d], piece_recv.at[line[d]], (b, line[d])).wait_recv()
+        own = own + pieces[line[d]]
+    blocks[b] = own
 
     count = [0]
 
     def pass_on(block, device):
-        send(blocks.at[block], blocks.at[block], block_send.at[count[0]], block_recv.at[block], (device, g))
+        piece = blocks.at[block]
+        send(piece, piece, block_send.at[count[0]], block_recv.at[block], (device, g))
         count[0] += 1
 
     def arrived(block):
-        remote(blocks.at[block], blocks.at[block], block_send.at[0], block_recv.at[block], (partner, g)).wait_recv()
-
-    for d in (1, 3, 2):
+        piece = blocks.at[block]
+        remote(piece, piece, block_send.at[0], block_recv.at[block], (partner, g)).wait_recv()
+
+    for d in (2, 1, 3):
         pass_on(b, along(d, 0))
-    for d in (1, 3, 2):
+    for d in (2, 1, 3):
         pass_on(b, along(0, d))
     pass_on(b, partner)
     for d in range(1, groups):
@@ -113,7 +119,7 @@
     for e in (1, 3, 2):
         block = along(e, 0)
         arrived(block)
-        for d in (1, 3, 2):
+        for d in (2, 1, 3):
             pass_on(block, along(0, d))
         pass_on(block, partner)
     for e in (0, 1, 3, 2):
@@ -125,45 +131,43 @@
     for i in range(SIDE * SIDE):
         arrived(2 * i + 1 - core)
 
-    for d in list(range(1, groups)) + [0]:
-        user = line[d]
+    for d in order + [0]:
         total = jnp.zeros((rows, WIN_BEAMS), jnp.float32)
         for k in range(slots):
-            weight = jnp.where(chosen[user, 0, slots + k] == g // 2, 1.0, 0.0)
-            total = total + weight * blocks[chosen[user, 0, k]]
+            wanted = chosen[line[d], 0, slots + k]
+            weight = jnp.where(wanted >= 0, 1.0, 0.0)
+            total = total + weight * blocks[chosen[line[d], 0, k], jnp.maximum(wanted, 0)]
         if d == 0:
-            parts[g] = total
+            out_ref[g] = total
         else:
-            sums[d] = total
-            send(sums.at[d], parts.at[g], part_send.at[d], part_recv.at[g], (b, user))
+            ready[d] = total
+            send(ready.at[d], sums.at[g], sum_send.at[d], sum_recv.at[g], (b, line[d]))
     for d in range(1, groups):
-        remote(sums.at[d], parts.at[line[d]], part_send.at[d], part_recv.at[line[d]], (b, line[d])).wait_recv()
-    for h in range(2):
-        total = parts[h]
-        for w in range(1, groups // 2):
-            total = total + parts[2 * w + h]
-        out_ref[h * rows : (h + 1) * rows, :] = total
+        piece = sums.at[line[d]]
+        remote(piece, piece, sum_send.at[d], sum_recv.at[line[d]], (b, line[d])).wait_recv()
+        out_ref[line[d]] = sums[line[d]]
     for copy in sent:
         copy.wait_send()
 
 
 def exchange(x, count, owner, window, groups, owners, slots):
-    rows = WIN_BEAMS // 2
+    windows, rows = x.shape[2] // WIN_BEAMS, WIN_BEAMS // groups
     vmem, smem = pl.BlockSpec(memory_space=pltpu.VMEM), pl.BlockSpec(memory_space=pltpu.SMEM)
     meta = (8, 128)
     dma = pltpu.SemaphoreType.DMA
     forwards = 2 * (SIDE - 1) + 1 + (SIDE - 1) * SIDE + SIDE * (SIDE - 1)
     return pl.pallas_call(
         functools.partial(exchange_kernel, groups, slots),
-        out_shape=jax.ShapeDtypeStruct((WIN_BEAMS, WIN_BEAMS), jnp.float32),
+        out_shape=jax.ShapeDtypeStruct((groups, rows, WIN_BEAMS), jnp.float32),
         in_specs=[vmem, smem, smem, smem],
         out_specs=vmem,
         scratch_shapes=[
             pltpu.VMEM(meta, jnp.int32),
-            pltpu.VMEM((groups,) + x.shape[:2] + (WIN_BEAMS,), x.dtype),
+            pltpu.VMEM((groups, windows, rows, WIN_BEAMS), jnp.float32),
+            pltpu.VMEM((groups, windows, rows, WIN_BEAMS), jnp.float32),
             pltpu.VMEM((groups,) + meta, jnp.int32),
             pltpu.SMEM((groups,) + meta, jnp.int32),
-            pltpu.VMEM((owners, rows, WIN_BEAMS), jnp.float32),
+            pltpu.VMEM((owners, windows, rows, WIN_BEAMS), jnp.float32),
             pltpu.VMEM((groups, rows, WIN_BEAMS), jnp.float32),
             pltpu.VMEM((groups, rows, WIN_BEAMS), jnp.float32),
             dma((groups,)),
@@ -178,14 +182,14 @@
         ],
         compiler_params=pltpu.CompilerParams(collective_id=0, has_side_effects=True),
         name="exchange",
-    )(x, count, owner, window)
-
-
+    )(x, count, owner, window).reshape(WIN_BEAMS, WIN_BEAMS)
+
+
+FAST = (2.4, -1.45, 0.0)
 GROW = (3.4445, -4.7750, 2.0315)
 CLOSE = ((3.109266, -3.792034, 1.535381), (1.90467, -1.282586, 0.3782733))
 LAST = (1.875, -1.25, 0.375)
-NEAR = 0.012
-ROUNDS = 8
+NEAR = 0.016
 PIECES = 8
 
 
@@ -222,7 +226,7 @@
 
 
 def finish_kernel(
-    beams_total, packed_ref, count_ref, grid_ref, out_ref, a_hi, a_lo, w_ref, gram_ref, c_hi, c_lo, length_ref
+    beams_total, packed_ref, count_ref, grid_ref, out_ref, a_hi, a_lo, start_ref, w_ref, gram_ref, c_hi, c_lo, length_ref
 ):
     n = WIN_BEAMS
     chunk = grid_ref.shape[1] // PIECES
@@ -245,7 +249,8 @@
     hi, lo = halves(shifted)
     a_hi[...] = hi
     a_lo[...] = lo
-    w_ref[...] = jnp.concatenate([shifted[:NOISE_DIM], shifted[n : n + NOISE_DIM]], axis=0)
+    start_ref[...] = jnp.concatenate([shifted[:NOISE_DIM], shifted[n : n + NOISE_DIM]], axis=0)
+    w_ref[...] = start_ref[...]
     eye = jnp.where(row == col, 1.0, 0.0)
 
     def steer(piece):
@@ -264,8 +269,10 @@
         a, b, c = coefs
         parts = halves(w_ref[...])
         gram = dot_nt(parts[0], parts[0])
-        low = gram.astype(jnp.bfloat16)
-        mix = a * eye + b * gram + c * dot(low, low)
+        mix = a * eye + b * gram
+        if c:
+            low = gram.astype(jnp.bfloat16)
+            mix = mix + c * dot(low, low)
         moved = halves(product(parts, (a_hi[...], a_lo[...]))) if apply_a else parts
         w_ref[...] = product_half(halves(mix), moved)
 
@@ -278,23 +285,29 @@
 
     @pl.loop(0, ITERS - 1)
     def _(i):
-        step(GROW, True)
+        step(FAST, True)
         steer(i)
 
     step(CLOSE[0])
     steer(ITERS - 1)
     step(CLOSE[1])
-
-    def again(state):
-        step(GROW)
+    off = distance()
+
+    @pl.when(jnp.logical_not(off < NEAR))
+    def _():
+        w_ref[...] = start_ref[...]
+
+        @pl.loop(0, ITERS - 1)
+        def _(_):
+            step(GROW)
+            step(CLOSE[0])
+            step(CLOSE[1], True)
+
         step(GROW)
         step(CLOSE[0])
         step(CLOSE[1])
-        return state[0] + 1, distance()
-
-    lax.while_loop(
-        lambda state: (state[1] > NEAR) & (state[0] < ROUNDS), again, (jnp.int32(0), distance())
-    )
+        distance()
+
     gram = gram_ref[...]
     parts = halves(gram)
     mix = LAST[0] * eye + LAST[1] * gram + LAST[2] * product_half(parts, parts)
@@ -321,6 +334,7 @@
             pltpu.VMEM((2 * n, 2 * n), jnp.bfloat16),
             pltpu.VMEM((2 * n, 2 * n), jnp.bfloat16),
             pltpu.VMEM((n, 2 * n), jnp.float32),
+            pltpu.VMEM((n, 2 * n), jnp.float32),
             pltpu.VMEM((n, n), jnp.float32),
             pltpu.VMEM((n, points), jnp.bfloat16),
             pltpu.VMEM((n, points), jnp.bfloat16),

time: 49.3 us -> 45 us (0.913)
  Pallas kernels: 48.5 us -> 44.1 us
    pallas_call x1, Pallas kernels: 38.7 us -> 35.5 us  [exchange(): pl.pallas_call(functools.partial(exchange_kernel, groups, slots), out_sha...]
    pallas_call x1, Pallas kernels: 9.81 us -> 8.61 us  [finish_user(): pl.pallas_call(functools.partial(finish_kernel, beams_total), out_shape=j...]
where the time goes in v4:
time: 45 us; the launch traced here: 44.8 us
  Pallas kernels  44.1 us (98%)
  between operations  0.66 us (1%)
    pallas_call x1, Pallas kernels, exchange(): pl.pallas_call(functools.partial(exchange_kernel, groups, slots), out_sha...  35.5 us
    pallas_call x1, Pallas kernels, finish_user(): pl.pallas_call(functools.partial(finish_kernel, beams_total), out_shape=j...  8.61 us

profile of v4, /device:TPU:1, one launch (start us, length us, event | category | flops | bytes accessed | tf_op | source)
XLA Modules:
  0.0 44.8 jit_solution(11765769035660648344)
XLA Ops:
  0.7 35.5 %exchange.1 = f32[8,16,128]{2,1,0:T(8,128)} custom-call(bf16[2,32,512]{2,1,0:T(8,128)(2,1)} %bitcast.4, s32[1]{0:T(128)S(6)} %copy.6.count_ref, s32[1,8]{1,0:T(1,128)} %bitcast.5, s32[1,8]{1,0:T(1,128)} %window_ref.1), custom_call_target="tpu_custom_call" | custom-call | tf_op jit(solution)/shard_map/exchange/pallas_call | solution.py:159
  36.2 8.6 %finish_user.1 = f32[1,4096]{1,0:T(1,128)} custom-call(f32[128,128]{1,0:T(8,128)} %bitcast.3, s32[1]{0:T(128)S(6)} %copy.6.count_ref, s32[1,4096]{1,0:T(1,128)} %grid_ref.1), custom_call_target="tpu_custom_call" | custom-call | tf_op jit(solution)/shard_map/finish_user/pallas_call | solution.py:328

commit v5 on v4

--- a/solution.py
+++ b/solution.py
@@ -37,8 +37,8 @@
 
 
 def exchange_kernel(
-    groups, slots, x_ref, count_ref, owner_ref, window_ref, out_ref, meta_ref, partial, pieces, metas, chosen, blocks,
-    ready, sums, piece_send, piece_recv, meta_send, meta_recv, block_send, block_recv, sum_send, sum_recv, local_sem,
+    groups, slots, x_hbm, count_ref, owner_hbm, window_hbm, out_ref, x_ref, owner_ref, window_ref, meta_ref, partial, pieces, metas, chosen, blocks,
+    ready, sums, piece_send, piece_recv, meta_send, meta_recv, block_send, block_recv, sum_send, sum_recv, local_sem, load_sem,
 ):
     b, g = lax.axis_index("beam"), lax.axis_index("grp")
     core, x, y = b % 2, b // (2 * SIDE), (b // 2) % SIDE
@@ -59,6 +59,16 @@
     for device in greeted:
         pl.semaphore_signal(barrier, inc=1, device_id=device, device_id_type=MESH)
 
+    loads = [
+        pltpu.make_async_copy(source, target, load_sem.at[i])
+        for i, (source, target) in enumerate(
+            [(x_hbm, x_ref), (owner_hbm, owner_ref), (window_hbm, window_ref)]
+        )
+    ]
+    for load in loads:
+        load.start()
+    for load in loads:
+        load.wait()
     lane = lax.broadcasted_iota(jnp.int32, meta_ref.shape, 1)
     meta = jnp.full(meta_ref.shape, -1, jnp.int32)
     for k in range(slots):
@@ -153,15 +163,19 @@
 def exchange(x, count, owner, window, groups, owners, slots):
     windows, rows = x.shape[2] // WIN_BEAMS, WIN_BEAMS // groups
     vmem, smem = pl.BlockSpec(memory_space=pltpu.VMEM), pl.BlockSpec(memory_space=pltpu.SMEM)
+    hbm = pl.BlockSpec(memory_space=pltpu.HBM)
     meta = (8, 128)
     dma = pltpu.SemaphoreType.DMA
     forwards = 2 * (SIDE - 1) + 1 + (SIDE - 1) * SIDE + SIDE * (SIDE - 1)
     return pl.pallas_call(
         functools.partial(exchange_kernel, groups, slots),
         out_shape=jax.ShapeDtypeStruct((groups, rows, WIN_BEAMS), jnp.float32),
-        in_specs=[vmem, smem, smem, smem],
+        in_specs=[hbm, smem, hbm, hbm],
         out_specs=vmem,
         scratch_shapes=[
+            pltpu.VMEM(x.shape, x.dtype),
+            pltpu.SMEM(owner.shape, owner.dtype),
+            pltpu.SMEM(window.shape, window.dtype),
             pltpu.VMEM(meta, jnp.int32),
             pltpu.VMEM((groups, windows, rows, WIN_BEAMS), jnp.float32),
             pltpu.VMEM((groups, windows, rows, WIN_BEAMS), jnp.float32),
@@ -179,6 +193,7 @@
             dma((groups,)),
             dma((groups,)),
             dma,
+            dma((3,)),
         ],
         compiler_params=pltpu.CompilerParams(collective_id=0, has_side_effects=True),
         name="exchange",
@@ -226,7 +241,7 @@
 
 
 def finish_kernel(
-    beams_total, packed_ref, count_ref, grid_ref, out_ref, a_hi, a_lo, start_ref, w_ref, gram_ref, c_hi, c_lo, length_ref
+    beams_total, packed_ref, count_ref, grid_ref, out_ref, a_hi, a_lo, b_hi, b_lo, start_ref, w_ref, gram_ref, c_hi, c_lo, length_ref
 ):
     n = WIN_BEAMS
     chunk = grid_ref.shape[1] // PIECES
@@ -250,7 +265,11 @@
     a_hi[...] = hi
     a_lo[...] = lo
     start_ref[...] = jnp.concatenate([shifted[:NOISE_DIM], shifted[n : n + NOISE_DIM]], axis=0)
-    w_ref[...] = start_ref[...]
+    twice = whole(product((hi[:n], lo[:n]), (hi, lo)))
+    hi, lo = halves(twice)
+    b_hi[...] = hi
+    b_lo[...] = lo
+    w_ref[...] = jnp.concatenate([twice[:NOISE_DIM], twice[n : n + NOISE_DIM]], axis=0)
     eye = jnp.where(row == col, 1.0, 0.0)
 
     def steer(piece):
@@ -265,7 +284,7 @@
         c_lo[:, where] = low
         length_ref[:, where] = jnp.sum(cot * cot, axis=0, keepdims=True) + n * slope * slope
 
-    def step(coefs, apply_a=False):
+    def step(coefs, operator=None):
         a, b, c = coefs
         parts = halves(w_ref[...])
         gram = dot_nt(parts[0], parts[0])
@@ -273,7 +292,7 @@
         if c:
             low = gram.astype(jnp.bfloat16)
             mix = mix + c * dot(low, low)
-        moved = halves(product(parts, (a_hi[...], a_lo[...]))) if apply_a else parts
+        moved = halves(product(parts, (operator[0][...], operator[1][...]))) if operator else parts
         w_ref[...] = product_half(halves(mix), moved)
 
     def distance():
@@ -283,13 +302,18 @@
         gram_ref[...] = gram
         return jnp.sum((gram - eye) * (gram - eye))
 
-    @pl.loop(0, ITERS - 1)
+    @pl.loop(0, ITERS // 2 - 1)
     def _(i):
-        step(FAST, True)
+        step(FAST, (b_hi, b_lo))
+        steer(2 * i)
+        steer(2 * i + 1)
+
+    @pl.loop(ITERS - 2, PIECES)
+    def _(i):
+        step(FAST)
         steer(i)
 
     step(CLOSE[0])
-    steer(ITERS - 1)
     step(CLOSE[1])
     off = distance()
 
@@ -301,7 +325,7 @@
         def _(_):
             step(GROW)
             step(CLOSE[0])
-            step(CLOSE[1], True)
+            step(CLOSE[1], (a_hi, a_lo))
 
         step(GROW)
         step(CLOSE[0])
@@ -333,6 +357,8 @@
         scratch_shapes=[
             pltpu.VMEM((2 * n, 2 * n), jnp.bfloat16),
             pltpu.VMEM((2 * n, 2 * n), jnp.bfloat16),
+            pltpu.VMEM((2 * n, 2 * n), jnp.bfloat16),
+            pltpu.VMEM((2 * n, 2 * n), jnp.bfloat16),
             pltpu.VMEM((n, 2 * n), jnp.float32),
             pltpu.VMEM((n, 2 * n), jnp.float32),
             pltpu.VMEM((n, n), jnp.float32),

time: 45 us -> 43.5 us (0.967)
  Pallas kernels: 44.1 us -> 42.6 us
    pallas_call x1, Pallas kernels: 35.5 us -> 34.7 us  [exchange(): pl.pallas_call(functools.partial(exchange_kernel, groups, slots), out_sha...]
    pallas_call x1, Pallas kernels: 8.61 us -> 7.93 us  [finish_user(): pl.pallas_call(functools.partial(finish_kernel, beams_total), out_shape=j...]
where the time goes in v5:
time: 43.5 us; the launch traced here: 43.3 us
  Pallas kernels  42.6 us (98%)
  between operations  0.66 us (2%)
    pallas_call x1, Pallas kernels, exchange(): pl.pallas_call(functools.partial(exchange_kernel, groups, slots), out_sha...  34.7 us
    pallas_call x1, Pallas kernels, finish_user(): pl.pallas_call(functools.partial(finish_kernel, beams_total), out_shape=j...  7.93 us

profile of v5, /device:TPU:1, one launch (start us, length us, event | category | flops | bytes accessed | tf_op | source)
XLA Modules:
  0.0 43.3 jit_solution(17553707446938088447)
XLA Ops:
  0.7 34.7 %exchange.1 = f32[8,16,128]{2,1,0:T(8,128)} custom-call(bf16[2,32,512]{2,1,0:T(8,128)(2,1)} %bitcast.4, s32[1]{0:T(128)S(6)} %copy.6.count_ref, s32[1,8]{1,0:T(1,128)} %bitcast.5, s32[1,8]{1,0:T(1,128)} %window_hbm.1), custom_call_target="tpu_custom_call" | custom-call | tf_op jit(solution)/shard_map/exchange/pallas_call | solution.py:170
  35.4 7.9 %finish_user.1 = f32[1,4096]{1,0:T(1,128)} custom-call(f32[128,128]{1,0:T(8,128)} %bitcast.3, s32[1]{0:T(128)S(6)} %copy.6.count_ref, s32[1,4096]{1,0:T(1,128)} %grid_ref.1), custom_call_target="tpu_custom_call" | custom-call | tf_op jit(solution)/shard_map/finish_user/pallas_call | solution.py:352

commit v6 on v5

--- a/solution.py
+++ b/solution.py
@@ -54,7 +54,9 @@
     order = sorted(range(1, groups), key=lambda d: -min(d, groups - d))
     barrier = pltpu.get_barrier_semaphore()
     greeted = [(b, line[d]) for d in order]
-    greeted += [(along(d, 0), g) for d in range(1, SIDE)] + [(along(0, d), g) for d in range(1, SIDE)]
+    steps = [(e, d) for e in range(SIDE) for d in range(SIDE) if e or d]
+    steps.sort(key=lambda s: -min(s[0], SIDE - s[0]) - min(s[1], SIDE - s[1]))
+    greeted += [(along(e, d), g) for e, d in steps]
     greeted += [(partner, g)]
     for device in greeted:
         pl.semaphore_signal(barrier, inc=1, device_id=device, device_id_type=MESH)
@@ -117,26 +119,17 @@
         piece = blocks.at[block]
         remote(piece, piece, block_send.at[0], block_recv.at[block], (partner, g)).wait_recv()
 
-    for d in (2, 1, 3):
-        pass_on(b, along(d, 0))
-    for d in (2, 1, 3):
-        pass_on(b, along(0, d))
     pass_on(b, partner)
+    for e, d in steps:
+        pass_on(b, along(e, d))
     for d in range(1, groups):
         remote(meta_ref, metas.at[line[d]], meta_send.at[d], meta_recv.at[line[d]], (b, line[d])).wait_recv()
     fetch = pltpu.make_async_copy(metas, chosen, local_sem)
     fetch.start()
-    for e in (1, 3, 2):
-        block = along(e, 0)
+    for e, d in reversed(steps):
+        block = along(e, d)
         arrived(block)
-        for d in (2, 1, 3):
-            pass_on(block, along(0, d))
         pass_on(block, partner)
-    for e in (0, 1, 3, 2):
-        for d in (1, 3, 2):
-            block = along(e, d)
-            arrived(block)
-            pass_on(block, partner)
     fetch.wait()
     for i in range(SIDE * SIDE):
         arrived(2 * i + 1 - core)
@@ -166,7 +159,7 @@
     hbm = pl.BlockSpec(memory_space=pltpu.HBM)
     meta = (8, 128)
     dma = pltpu.SemaphoreType.DMA
-    forwards = 2 * (SIDE - 1) + 1 + (SIDE - 1) * SIDE + SIDE * (SIDE - 1)
+    forwards = 2 * SIDE * SIDE - 1
     return pl.pallas_call(
         functools.partial(exchange_kernel, groups, slots),
         out_shape=jax.ShapeDtypeStruct((groups, rows, WIN_BEAMS), jnp.float32),

time: 43.5 us -> 42.2 us (0.970)
  Pallas kernels: 42.6 us -> 41.3 us
    pallas_call x1, Pallas kernels: 34.7 us -> 33.4 us  [exchange(): pl.pallas_call(functools.partial(exchange_kernel, groups, slots), out_sha...]
where the time goes in v6:
time: 42.2 us; the launch traced here: 42 us
  Pallas kernels  41.3 us (98%)
  between operations  0.66 us (2%)
    pallas_call x1, Pallas kernels, exchange(): pl.pallas_call(functools.partial(exchange_kernel, groups, slots), out_sha...  33.4 us
    pallas_call x1, Pallas kernels, finish_user(): pl.pallas_call(functools.partial(finish_kernel, beams_total), out_shape=j...  7.93 us

profile of v6, /device:TPU:1, one launch (start us, length us, event | category | flops | bytes accessed | tf_op | source)
XLA Modules:
  0.0 42.0 jit_solution(13180027863226625633)
XLA Ops:
  0.7 33.4 %exchange.1 = f32[8,16,128]{2,1,0:T(8,128)} custom-call(bf16[2,32,512]{2,1,0:T(8,128)(2,1)} %bitcast.4, s32[1]{0:T(128)S(6)} %copy.6.count_ref, s32[1,8]{1,0:T(1,128)} %bitcast.5, s32[1,8]{1,0:T(1,128)} %window_hbm.1), custom_call_target="tpu_custom_call" | custom-call | tf_op jit(solution)/shard_map/exchange/pallas_call | solution.py:163
  34.1 7.9 %finish_user.1 = f32[1,4096]{1,0:T(1,128)} custom-call(f32[128,128]{1,0:T(8,128)} %bitcast.3, s32[1]{0:T(128)S(6)} %copy.6.count_ref, s32[1,4096]{1,0:T(1,128)} %grid_ref.1), custom_call_target="tpu_custom_call" | custom-call | tf_op jit(solution)/shard_map/finish_user/pallas_call | solution.py:345

commit v7 on v6

--- a/solution.py
+++ b/solution.py
@@ -96,43 +96,49 @@
         copy.start()
         sent.append(copy)
 
-    for d in order:
-        send(partial.at[line[d]], pieces.at[g], piece_send.at[d], piece_recv.at[g], (b, line[d]))
+    halves_of = [pl.ds(p * (windows // 2), windows // 2) for p in range(2)]
+    for p, part in enumerate(halves_of):
+        for d in order:
+            target = pieces.at[g, part]
+            send(partial.at[line[d], part], target, piece_send.at[p, d], piece_recv.at[p, g], (b, line[d]))
     for d in order:
         send(meta_ref, metas.at[g], meta_send.at[d], meta_recv.at[g], (b, line[d]))
     metas[g] = meta_ref[...]
-    own = partial[g]
-    for d in reversed(order):
-        piece = pieces.at[line[d]]
-        remote(piece, piece, piece_send.at[d], piece_recv.at[line[d]], (b, line[d])).wait_recv()
-        own = own + pieces[line[d]]
-    blocks[b] = own
 
     count = [0]
 
-    def pass_on(block, device):
-        piece = blocks.at[block]
-        send(piece, piece, block_send.at[count[0]], block_recv.at[block], (device, g))
+    def pass_on(p, block, device):
+        piece = blocks.at[block, halves_of[p]]
+        send(piece, piece, block_send.at[count[0]], block_recv.at[p, block], (device, g))
         count[0] += 1
 
-    def arrived(block):
-        piece = blocks.at[block]
-        remote(piece, piece, block_send.at[0], block_recv.at[block], (partner, g)).wait_recv()
-
-    pass_on(b, partner)
-    for e, d in steps:
-        pass_on(b, along(e, d))
+    def arrived(p, block):
+        piece = blocks.at[block, halves_of[p]]
+        remote(piece, piece, block_send.at[0], block_recv.at[p, block], (partner, g)).wait_recv()
+
+    for p, part in enumerate(halves_of):
+        own = partial[g, part]
+        for d in reversed(order):
+            piece = pieces.at[line[d], part]
+            remote(piece, piece, piece_send.at[p, d], piece_recv.at[p, line[d]], (b, line[d])).wait_recv()
+            own = own + pieces[line[d], part]
+        blocks[b, part] = own
+        pass_on(p, b, partner)
+        for e, d in steps:
+            pass_on(p, b, along(e, d))
     for d in range(1, groups):
         remote(meta_ref, metas.at[line[d]], meta_send.at[d], meta_recv.at[line[d]], (b, line[d])).wait_recv()
     fetch = pltpu.make_async_copy(metas, chosen, local_sem)
     fetch.start()
-    for e, d in reversed(steps):
-        block = along(e, d)
-        arrived(block)
-        pass_on(block, partner)
+    for p in range(2):
+        for e, d in reversed(steps):
+            block = along(e, d)
+            arrived(p, block)
+            pass_on(p, block, partner)
     fetch.wait()
-    for i in range(SIDE * SIDE):
-        arrived(2 * i + 1 - core)
+    for p in range(2):
+        for i in range(SIDE * SIDE):
+            arrived(p, 2 * i + 1 - core)
 
     for d in order + [0]:
         total = jnp.zeros((rows, WIN_BEAMS), jnp.float32)
@@ -159,7 +165,7 @@
     hbm = pl.BlockSpec(memory_space=pltpu.HBM)
     meta = (8, 128)
     dma = pltpu.SemaphoreType.DMA
-    forwards = 2 * SIDE * SIDE - 1
+    forwards = 2 * (2 * SIDE * SIDE - 1)
     return pl.pallas_call(
         functools.partial(exchange_kernel, groups, slots),
         out_shape=jax.ShapeDtypeStruct((groups, rows, WIN_BEAMS), jnp.float32),
@@ -177,12 +183,12 @@
             pltpu.VMEM((owners, windows, rows, WIN_BEAMS), jnp.float32),
             pltpu.VMEM((groups, rows, WIN_BEAMS), jnp.float32),
             pltpu.VMEM((groups, rows, WIN_BEAMS), jnp.float32),
-            dma((groups,)),
-            dma((groups,)),
+            dma((2, groups)),
+            dma((2, groups)),
             dma((groups,)),
             dma((groups,)),
             dma((forwards,)),
-            dma((owners,)),
+            dma((2, owners)),
             dma((groups,)),
             dma((groups,)),
             dma,

time: 42.2 us -> 40.8 us (0.967)
  Pallas kernels: 41.3 us -> 40 us
    pallas_call x1, Pallas kernels: 33.4 us -> 32.1 us  [exchange(): pl.pallas_call(functools.partial(exchange_kernel, groups, slots), out_sha...]
where the time goes in v7:
time: 40.8 us; the launch traced here: 40.7 us
  Pallas kernels  40 us (98%)
  between operations  0.66 us (2%)
    pallas_call x1, Pallas kernels, exchange(): pl.pallas_call(functools.partial(exchange_kernel, groups, slots), out_sha...  32.1 us
    pallas_call x1, Pallas kernels, finish_user(): pl.pallas_call(functools.partial(finish_kernel, beams_total), out_shape=j...  7.93 us

profile of v7, /device:TPU:1, one launch (start us, length us, event | category | flops | bytes accessed | tf_op | source)
XLA Modules:
  0.0 40.7 jit_solution(15837203478602685268)
XLA Ops:
  0.7 32.1 %exchange.1 = f32[8,16,128]{2,1,0:T(8,128)} custom-call(bf16[2,32,512]{2,1,0:T(8,128)(2,1)} %bitcast.4, s32[1]{0:T(128)S(6)} %copy.6.count_ref, s32[1,8]{1,0:T(1,128)} %bitcast.5, s32[1,8]{1,0:T(1,128)} %window_hbm.1), custom_call_target="tpu_custom_call" | custom-call | tf_op jit(solution)/shard_map/exchange/pallas_call | solution.py:169
  32.7 7.9 %finish_user.1 = f32[1,4096]{1,0:T(1,128)} custom-call(f32[128,128]{1,0:T(8,128)} %bitcast.3, s32[1]{0:T(128)S(6)} %copy.6.count_ref, s32[1,4096]{1,0:T(1,128)} %grid_ref.1), custom_call_target="tpu_custom_call" | custom-call | tf_op jit(solution)/shard_map/finish_user/pallas_call | solution.py:351

commit v8 on v7

--- a/solution.py
+++ b/solution.py
@@ -272,7 +272,7 @@
     eye = jnp.where(row == col, 1.0, 0.0)
 
     def steer(piece):
-        where = pl.ds(pl.multiple_of(piece * chunk, chunk), chunk)
+        where = slice(piece * chunk, (piece + 1) * chunk)
         position = (grid_ref[:, where].astype(jnp.float32) + 0.5) / OVERSAMPLE
         offset = position - lax.broadcasted_iota(jnp.int32, (n, chunk), 0).astype(jnp.float32)
         angle = (slope * offset) * (slope * offset)
@@ -301,14 +301,12 @@
         gram_ref[...] = gram
         return jnp.sum((gram - eye) * (gram - eye))
 
-    @pl.loop(0, ITERS // 2 - 1)
-    def _(i):
+    for i in range(ITERS // 2 - 1):
         step(FAST, (b_hi, b_lo))
         steer(2 * i)
         steer(2 * i + 1)
 
-    @pl.loop(ITERS - 2, PIECES)
-    def _(i):
+    for i in range(ITERS - 2, PIECES):
         step(FAST)
         steer(i)
 

time: 40.8 us -> 40.6 us (level)
  no operation moved by 1% of the time
where the time goes in v8:
time: 40.6 us; the launch traced here: 40.4 us
  Pallas kernels  39.8 us (98%)
  between operations  0.66 us (2%)
    pallas_call x1, Pallas kernels, exchange(): pl.pallas_call(functools.partial(exchange_kernel, groups, slots), out_sha...  32.1 us
    pallas_call x1, Pallas kernels, finish_user(): pl.pallas_call(functools.partial(finish_kernel, beams_total), out_shape=j...  7.69 us

profile of v8, /device:TPU:1, one launch (start us, length us, event | category | flops | bytes accessed | tf_op | source)
XLA Modules:
  0.0 40.4 jit_solution(6979018215380644564)
XLA Ops:
  0.7 32.1 %exchange.1 = f32[8,16,128]{2,1,0:T(8,128)} custom-call(bf16[2,32,512]{2,1,0:T(8,128)(2,1)} %bitcast.4, s32[1]{0:T(128)S(6)} %copy.6.count_ref, s32[1,8]{1,0:T(1,128)} %bitcast.5, s32[1,8]{1,0:T(1,128)} %window_hbm.1), custom_call_target="tpu_custom_call" | custom-call | tf_op jit(solution)/shard_map/exchange/pallas_call | solution.py:169
  32.7 7.7 %finish_user.1 = f32[1,4096]{1,0:T(1,128)} custom-call(f32[128,128]{1,0:T(8,128)} %bitcast.3, s32[1]{0:T(128)S(6)} %copy.6.count_ref, s32[1,4096]{1,0:T(1,128)} %grid_ref.1), custom_call_target="tpu_custom_call" | custom-call | tf_op jit(solution)/shard_map/finish_user/pallas_call | solution.py:349

commit v9 on v7

--- a/solution.py
+++ b/solution.py
@@ -253,8 +253,23 @@
     imag = jnp.where(row > col, packed, jnp.where(row < col, -flipped, 0.0))
     scale = jnp.full((1, 1), 1.0, jnp.float32) / (count_ref[0].astype(jnp.float32) * SNAPS)
     top = jnp.concatenate([same, -imag], axis=1) * scale
+    def steer(piece):
+        where = slice(piece * chunk, (piece + 1) * chunk)
+        position = (grid_ref[:, where].astype(jnp.float32) + 0.5) / OVERSAMPLE
+        offset = position - lax.broadcasted_iota(jnp.int32, (n, chunk), 0).astype(jnp.float32)
+        angle = (slope * offset) * (slope * offset)
+        series = 1.0 / 3.0 + angle * (1.0 / 45.0 + angle * (2.0 / 945.0))
+        cot = 1.0 / offset - (slope * slope * offset) * series
+        high, low = halves(cot)
+        c_hi[:, where] = high
+        c_lo[:, where] = low
+        length_ref[:, where] = jnp.sum(cot * cot, axis=0, keepdims=True) + n * slope * slope
+
     square = product(halves(top), halves(whole(top)))
+    steer(0)
+    steer(1)
     fourth = product(halves(square), halves(whole(square)))
+    steer(2)
     power = 2.0 * jnp.sum(fourth * fourth, axis=(0, 1), keepdims=True)
     shift = shift_factor * jnp.sqrt(jnp.sqrt(jnp.sqrt(power)))
     row2 = lax.broadcasted_iota(jnp.int32, (n, 2 * n), 0)
@@ -265,23 +280,12 @@
     a_lo[...] = lo
     start_ref[...] = jnp.concatenate([shifted[:NOISE_DIM], shifted[n : n + NOISE_DIM]], axis=0)
     twice = whole(product((hi[:n], lo[:n]), (hi, lo)))
+    steer(3)
     hi, lo = halves(twice)
     b_hi[...] = hi
     b_lo[...] = lo
     w_ref[...] = jnp.concatenate([twice[:NOISE_DIM], twice[n : n + NOISE_DIM]], axis=0)
     eye = jnp.where(row == col, 1.0, 0.0)
-
-    def steer(piece):
-        where = pl.ds(pl.multiple_of(piece * chunk, chunk), chunk)
-        position = (grid_ref[:, where].astype(jnp.float32) + 0.5) / OVERSAMPLE
-        offset = position - lax.broadcasted_iota(jnp.int32, (n, chunk), 0).astype(jnp.float32)
-        angle = (slope * offset) * (slope * offset)
-        series = 1.0 / 3.0 + angle * (1.0 / 45.0 + angle * (2.0 / 945.0))
-        cot = 1.0 / offset - (slope * slope * offset) * series
-        high, low = halves(cot)
-        c_hi[:, where] = high
-        c_lo[:, where] = low
-        length_ref[:, where] = jnp.sum(cot * cot, axis=0, keepdims=True) + n * slope * slope
 
     def step(coefs, operator=None):
         a, b, c = coefs
@@ -301,16 +305,13 @@
         gram_ref[...] = gram
         return jnp.sum((gram - eye) * (gram - eye))
 
-    @pl.loop(0, ITERS // 2 - 1)
-    def _(i):
+    for i in range(ITERS // 2 - 1):
         step(FAST, (b_hi, b_lo))
-        steer(2 * i)
-        steer(2 * i + 1)
-
-    @pl.loop(ITERS - 2, PIECES)
-    def _(i):
-        step(FAST)
-        steer(i)
+        steer(4 + i)
+
+    step(FAST)
+    steer(PIECES - 1)
+    step(FAST)
 
     step(CLOSE[0])
     step(CLOSE[1])

time: 40.8 us -> 40.6 us (level)
  no operation moved by 1% of the time
where the time goes in v9:
time: 40.6 us; the launch traced here: 40.4 us
  Pallas kernels  39.8 us (98%)
  between operations  0.66 us (2%)
    pallas_call x1, Pallas kernels, exchange(): pl.pallas_call(functools.partial(exchange_kernel, groups, slots), out_sha...  32.1 us
    pallas_call x1, Pallas kernels, finish_user(): pl.pallas_call(functools.partial(finish_kernel, beams_total), out_shape=j...  7.69 us

profile of v9, /device:TPU:1, one launch (start us, length us, event | category | flops | bytes accessed | tf_op | source)
XLA Modules:
  0.0 40.4 jit_solution(13765782021067329150)
XLA Ops:
  0.7 32.1 %exchange.1 = f32[8,16,128]{2,1,0:T(8,128)} custom-call(bf16[2,32,512]{2,1,0:T(8,128)(2,1)} %bitcast.4, s32[1]{0:T(128)S(6)} %copy.6.count_ref, s32[1,8]{1,0:T(1,128)} %bitcast.5, s32[1,8]{1,0:T(1,128)} %window_hbm.1), custom_call_target="tpu_custom_call" | custom-call | tf_op jit(solution)/shard_map/exchange/pallas_call | solution.py:169
  32.7 7.7 %finish_user.1 = f32[1,4096]{1,0:T(1,128)} custom-call(f32[128,128]{1,0:T(8,128)} %bitcast.3, s32[1]{0:T(128)S(6)} %copy.6.count_ref, s32[1,4096]{1,0:T(1,128)} %grid_ref.1), custom_call_target="tpu_custom_call" | custom-call | tf_op jit(solution)/shard_map/finish_user/pallas_call | solution.py:352
